TPU v7x, 64 devices: a 2x2x8 block of a 4x4x8 slice. The times are simulated.
64 devices in a mesh: dp: 4 (over x, y), tp: 16 (over z, core).
Axes of the slice: x: 2, y: 2, z: 8, core: 2. Of those that a mesh axis runs over, the one named last changes fastest.
The devices are a block of a 4x4x8 slice.
Arguments:
- tokens_in: bfloat16 [128, 256, 1024], P('dp'), parts along dimension 0
- ln_scale: bfloat16 [2, 1024], replicated
- w_query: bfloat16 [2, 1024, 1024], P(None, None, 'tp')
- w_key: bfloat16 [2, 1024, 1024], P(None, None, 'tp')
- w_value: bfloat16 [2, 1024, 1024], P(None, None, 'tp')
- q_scale: bfloat16 [2, 64], replicated
- k_scale: bfloat16 [2, 64], replicated
- w_out: bfloat16 [2, 1024, 1024], P(None, 'tp')
- b_out: bfloat16 [2, 1024], replicated
- w_up: bfloat16 [2, 1024, 4096], P(None, None, 'tp')
- b_up: bfloat16 [2, 4096], P(None, 'tp')
- w_down: bfloat16 [2, 4096, 1024], P(None, 'tp')
- b_down: bfloat16 [2, 1024], replicated
Outputs:
- output: bfloat16 [128, 256, 1024], P('dp'), parts along dimension 0
There are 4 independent parts. A program takes and returns all parts, laid end to end along the dimension named above; an argument that names none is the same for every part.
All inputs are finite; a program needn't handle non-finite values.
Results may differ from a plain program's by a relative error of at most 0.0156837.
Values are sent between devices in bfloat16 or wider.
A program may use at most 768 MiB of HBM per device.

v0:
```python
import jax
import jax.numpy as jnp
from jax import lax
from jax.sharding import PartitionSpec as P

LN_EPS = 1e-6


def layer_norm(values, scale_vec):
    mean_val = jnp.mean(values, axis=-1, keepdims=True)
    centered = values - mean_val
    variance = jnp.mean(centered * centered, axis=-1, keepdims=True)
    return centered * lax.rsqrt(variance + LN_EPS) * scale_vec.astype(jnp.float32)


def local_branches(normed, n_images, seq_len, w_query, w_key, w_value, q_scale, k_scale, w_out, w_up, b_up, w_down):
    head_dim = q_scale.shape[0]
    local_heads = w_query.shape[1] // head_dim

    def project(weight):
        projected = jnp.dot(normed, weight, preferred_element_type=jnp.float32)
        return projected.reshape(n_images, seq_len, local_heads, head_dim)

    queries = layer_norm(project(w_query), q_scale).astype(jnp.bfloat16)
    keys_all = layer_norm(project(w_key), k_scale).astype(jnp.bfloat16)
    values_all = project(w_value).astype(jnp.bfloat16)
    scores = jnp.einsum("bqhd,bkhd->bhqk", queries, keys_all, preferred_element_type=jnp.float32) * head_dim ** -0.5
    attn_prob = jax.nn.softmax(scores, axis=-1).astype(jnp.bfloat16)
    mixed_val = jnp.einsum("bhqk,bkhd->bqhd", attn_prob, values_all, preferred_element_type=jnp.float32)
    mixed_val = mixed_val.astype(jnp.bfloat16).reshape(n_images * seq_len, local_heads * head_dim)
    attn_part = jnp.dot(mixed_val, w_out, preferred_element_type=jnp.float32)
    pre_act = jnp.dot(normed, w_up, preferred_element_type=jnp.float32) + b_up.astype(jnp.float32)
    activated = jax.nn.gelu(pre_act, approximate=True).astype(jnp.bfloat16)
    return attn_part + jnp.dot(activated, w_down, preferred_element_type=jnp.float32)


def solution(mesh):
    col_spec = P(None, None, "tp")
    row_spec = P(None, "tp", None)
    in_specs = (P("dp", None, None), P(), col_spec, col_spec, col_spec, P(), P(), row_spec, P(), col_spec, P(None, "tp"), row_spec, P())

    def per_device(tokens_in, ln_scale, w_query, w_key, w_value, q_scale, k_scale, w_out, b_out, w_up, b_up, w_down, b_down):
        n_images, seq_len, model_dim = tokens_in.shape
        n_tokens = n_images * seq_len
        current = tokens_in
        for layer_idx in range(w_query.shape[0]):
            residual = current.reshape(n_tokens, model_dim).astype(jnp.float32)
            normed = layer_norm(residual, ln_scale[layer_idx]).astype(jnp.bfloat16)
            part_sum = local_branches(normed, n_images, seq_len, w_query[layer_idx], w_key[layer_idx], w_value[layer_idx], q_scale[layer_idx], k_scale[layer_idx], w_out[layer_idx], w_up[layer_idx], b_up[layer_idx], w_down[layer_idx])
            reduced = lax.psum(part_sum.astype(jnp.bfloat16), "tp")
            summed = residual + b_out[layer_idx].astype(jnp.float32) + b_down[layer_idx].astype(jnp.float32) + reduced.astype(jnp.float32)
            current = summed.astype(jnp.bfloat16).reshape(n_images, seq_len, model_dim)
        return current

    return jax.shard_map(per_device, mesh=mesh, in_specs=in_specs, out_specs=P("dp", None, None), check_vma=False)
```

profile of v0, /device:TPU:21, one launch (start us, length us, event | category | flops | bytes accessed | tf_op | source)
XLA Modules:
  0.0 640.1 jit_solution(13734859285129236972)
XLA Ops:
  6.5 0.0 all-reduce.3.cloned.1.call-start
  6.6 1.3 slice_convert_fusion.6
  7.9 0.8 slice_convert_fusion
  8.7 7.0 %convert_reduce_fusion.1 = f32[32,256]{1,0:T(8,128)S(1)} fusion(bf16[32,256,1024]{2,1,0:T(8,128)(2,1)} %param.13), kind=kLoop, calls=%fused_computation.21 | loop fusion | flops 16769024 | bytes 16809984 | tf_op jit(solution)/shard_map/reduce_sum | solution.py:10
  15.7 3.6 copy-done
  19.3 5.6 multiply_reduce_fusion
  25.0 0.0 copy-start.4
  25.0 5.6 multiply_convert_fusion
  30.6 0.0 copy-start.2
  30.6 0.0 copy-done.4
  30.6 0.0 copy-start.5
  30.6 5.3 fusion.122
  35.9 0.9 copy-done.2
  36.8 0.3 multiply_reduce_fusion.5
  37.1 0.0 copy-done.5
  37.1 0.0 copy-start.9
  37.1 0.0 copy-start.10
  37.1 12.3 %fusion.123 = (f32[8192]{0:T(1024)S(1)}, f32[8192,64]{0,1:T(8,128)}) fusion(bf16[8192,1024]{1,0:T(8,128)(2,1)} %bitcast.163, bf16[2,1024,64]{1,2,0:T(8,128)(2,1)S(1)} %copy-done.5), kind=kOutput, calls=%fused_computation.159 | convolution fusion | flops 1074257920 | bytes 19038208 | tf_op jit(solution)/shard_map/dot_general | solution.py:21
  49.5 1.9 multiply_reduce_fusion.6
  51.4 0.0 copy-done.9
  51.4 0.0 copy-done.10
  51.4 3.0 fusion.55
  54.4 0.0 copy-start.15
  54.4 4.7 fusion.124
  59.2 0.0 copy-done.15
  59.2 0.0 copy-start.6
  59.2 14.1 %fusion.131 = bf16[8,8,32,256]{3,1,0,2:T(8,128)(2,1)S(1)} fusion(f32[32,256,256]{1,2,0:T(8,128)} %get-tuple-element.24, f32[32,256]{1,0:T(8,128)S(1)} %get-tuple-element.23, bf16[32,256,1024]{2,1,0:T(8,128)(2,1)} %copy-done.2, bf16[2,1024,64]{1,2,0:T(8,128)(2,1)S(1)} %copy-done.15), kind=kOutput, calls=%fused_computation.165 | convolution fusion | flops 1347420160 | bytes 26378240 | tf_op jit(solution)/shard_map/bhqk,bkhd->bqhd/dot_general | solution.py:29
  73.3 0.1 copy.34
  73.4 0.0 copy-done.6
  73.4 0.0 copy-start.12
  73.4 13.1 %fusion.93 = f32[8192,1024]{1,0:T(8,128)} fusion(bf16[8192,64]{0,1:T(8,128)(2,1)S(1)} %bitcast.170, bf16[2,64,1024]{2,1,0:T(8,128)(2,1)S(1)} %copy-done.6), kind=kOutput, calls=%fused_computation.109 | convolution fusion | flops 1073741824 | bytes 34734080 | tf_op jit(solution)/shard_map/dot_general | solution.py:31
  86.5 0.0 copy-done.12
  86.5 27.8 %add_convert_fusion.1 = bf16[8192,1024]{1,0:T(8,128)(2,1)} fusion(f32[8192,1024]{1,0:T(8,128)} %fusion.93, bf16[8192,1024]{1,0:T(8,128)(2,1)} %bitcast.164, f32[256]{0:T(256)S(1)} %bitcast.179, bf16[2,256,1024]{2,1,0:T(8,128)(2,1)S(1)} %copy-done.12, bf16[2,1024,256]{2,1,0:T(8,128)(2,1)} %param.22), kind=kOutput, calls=%fused_computation.18 | convolution fusion | flops 8627683328 | bytes 68158464 | tf_op jit(solution)/shard_map/dot_general | solution.py:34
  114.3 0.1 all-reduce.3.cloned.1.call-update
  114.4 0.1 all-reduce.5.cloned.1.call-start
  114.4 0.5 copy-done.7
  115.0 0.0 copy-done.8
  115.0 196.5 %all-reduce.3.cloned.1.call-done = bf16[8192,1024]{1,0:T(8,128)(2,1)} async-done(((bf16[8192,1024]{1,0:T(8,128)(2,1)}), bf16[8192,1024]{1,0:T(8,128)(2,1)}) %all-reduce.3.cloned.1.call-update) | async-done | bytes 16777232 | tf_op jit(solution)/shard_map/psum | solution.py:50
  311.5 15.6 %convert_reduce_fusion = (f32[8192]{0:T(1024)S(1)}, bf16[8192,1024]{1,0:T(8,128)(2,1)S(1)}) fusion(bf16[8192,1024]{1,0:T(8,128)(2,1)} %all-reduce.3.cloned.1.call-done, f32[1024]{0:T(1024)S(1)} %bitcast.174, f32[1024]{0:T(1024)S(1)} %bitcast.173, bf16[32,256,1024]{2,1,0:T(8,128)(2,1)} %param.13), kind=kLoop, calls=%fused_computation.3 | loop fusion | flops 67100672 | bytes 50372608 | tf_op jit(solution)/shard_map/reduce_sum | solution.py:10
  327.1 0.0 copy-start.1
  327.2 5.6 fusion.4
  332.8 0.5 copy-done.1
  333.3 5.7 fusion.6
  339.0 0.0 copy-start.3
  339.0 6.6 %fusion.125 = (f32[8192]{0:T(1024)S(1)}, f32[8192,64]{0,1:T(8,128)}) fusion(bf16[8192,1024]{1,0:T(8,128)(2,1)S(1)} %fusion.6, bf16[2,1024,64]{1,2,0:T(8,128)(2,1)S(1)} %copy-done.4), kind=kOutput, calls=%fused_computation.161 | convolution fusion | flops 1074257920 | bytes 19038208 | tf_op jit(solution)/shard_map/dot_general | solution.py:21
  345.6 0.0 copy-done.3
  345.6 6.6 %fusion.126 = (f32[8192]{0:T(1024)S(1)}, f32[8192,64]{0,1:T(8,128)}) fusion(bf16[8192,1024]{1,0:T(8,128)(2,1)S(1)} %fusion.6, bf16[2,1024,64]{1,2,0:T(8,128)(2,1)S(1)} %copy-done.5), kind=kOutput, calls=%fused_computation.162 | convolution fusion | flops 1074257920 | bytes 19038208 | tf_op jit(solution)/shard_map/dot_general | solution.py:21
  352.2 1.9 multiply_reduce_fusion.3
  354.1 1.9 multiply_reduce_fusion.4
  356.0 3.6 fusion.58
  359.6 4.6 fusion.127
  364.2 14.1 %fusion.128 = bf16[8,8,32,256]{3,1,0,2:T(8,128)(2,1)S(1)} fusion(f32[32,256,256]{1,2,0:T(8,128)} %get-tuple-element.30, f32[32,256]{1,0:T(8,128)S(1)} %get-tuple-element.29, bf16[32,256,1024]{2,1,0:T(8,128)(2,1)} %bitcast.165, bf16[2,1024,64]{1,2,0:T(8,128)(2,1)S(1)} %copy-done.15), kind=kOutput, calls=%fused_computation.164 | convolution fusion | flops 1347420160 | bytes 26378240 | tf_op jit(solution)/shard_map/bhqk,bkhd->bqhd/dot_general | solution.py:29
  378.3 0.1 copy.35
  378.4 0.0 copy-start.11
  378.4 0.0 copy-start.13
  378.4 0.0 copy-start.14
  378.4 13.1 %fusion.85 = f32[8192,1024]{1,0:T(8,128)} fusion(bf16[8192,64]{0,1:T(8,128)(2,1)S(1)} %bitcast.171, bf16[2,64,1024]{2,1,0:T(8,128)(2,1)S(1)} %copy-done.6), kind=kOutput, calls=%fused_computation.102 | convolution fusion | flops 1073741824 | bytes 34734080 | tf_op jit(solution)/shard_map/dot_general | solution.py:31
  391.5 0.0 copy-done.11
  391.5 0.0 copy-done.13
  391.5 0.0 copy-done.14
  391.5 29.9 %add_convert_fusion = bf16[8192,1024]{1,0:T(8,128)(2,1)} fusion(f32[8192,1024]{1,0:T(8,128)} %fusion.85, bf16[8192,1024]{1,0:T(8,128)(2,1)} %copy-done.3, f32[256]{0:T(256)S(1)} %bitcast.178, bf16[2,256,1024]{2,1,0:T(8,128)(2,1)S(1)} %copy-done.13, bf16[2,1024,256]{2,1,0:T(8,128)(2,1)S(1)} %copy-done.14), kind=kOutput, calls=%fused_computation.17 | convolution fusion | flops 8627683328 | bytes 68158464 | tf_op jit(solution)/shard_map/dot_general | solution.py:34
  421.5 0.1 all-reduce.5.cloned.1.call-update
  421.5 191.7 %all-reduce.5.cloned.1.call-done = bf16[8192,1024]{1,0:T(8,128)(2,1)} async-done(((bf16[8192,1024]{1,0:T(8,128)(2,1)}), bf16[8192,1024]{1,0:T(8,128)(2,1)}) %all-reduce.5.cloned.1.call-update) | async-done | bytes 16777232 | tf_op jit(solution)/shard_map/psum | solution.py:50
  613.3 19.5 %fusion.9 = bf16[8192,1024]{1,0:T(8,128)(2,1)} fusion(bf16[8192,1024]{1,0:T(8,128)(2,1)} %copy-done.1, bf16[8192,1024]{1,0:T(8,128)(2,1)} %all-reduce.5.cloned.1.call-done, f32[1024]{0:T(1024)S(1)} %bitcast.177, f32[1024]{0:T(1024)S(1)} %bitcast.176), kind=kLoop, calls=%fused_computation.12 | loop fusion | flops 50331648 | bytes 50339840 | tf_op jit(solution)/shard_map/convert_element_type | solution.py:52
  (26 shorter events, 0.2 us)
Async XLA Ops:
  6.5 305.0 %all-reduce.3.cloned.1.call-start = ((), (), s32[]{:S(2)}) async-start(), calls=%async_computation | async-start | bytes 33554432 | tf_op jit(solution)/shard_map/psum | solution.py:50
  8.7 10.7 %copy-start = (bf16[32,256,1024]{2,1,0:T(8,128)(2,1)S(1)}, bf16[32,256,1024]{2,1,0:T(8,128)(2,1)}, u32[]{:S(2)}) copy-start(bf16[32,256,1024]{2,1,0:T(8,128)(2,1)} %param.13) | copy-start | bytes 50331652
  25.0 5.6 copy-start.4
  30.6 6.2 copy-start.2
  30.6 6.5 %copy-start.5 = (bf16[2,1024,64]{1,2,0:T(8,128)(2,1)S(1)}, bf16[2,1024,64]{1,2,0:T(8,128)(2,1)}, u32[]{:S(2)}) copy-start(bf16[2,1024,64]{1,2,0:T(8,128)(2,1)} %param.15) | copy-start | bytes 786436
  37.1 14.3 %copy-start.9 = (bf16[2,64]{1,0:T(2,128)(2,1)S(1)}, bf16[2,64]{1,0:T(2,128)(2,1)}, u32[]{:S(2)}) copy-start(bf16[2,64]{1,0:T(2,128)(2,1)} %param.19) | copy-start | bytes 772
  37.1 14.3 %copy-start.10 = (bf16[2,64]{1,0:T(2,128)(2,1)S(1)}, bf16[2,64]{1,0:T(2,128)(2,1)}, u32[]{:S(2)}) copy-start(bf16[2,64]{1,0:T(2,128)(2,1)} %param.18) | copy-start | bytes 772
  54.4 4.8 copy-start.15
  59.2 14.2 %copy-start.6 = (bf16[2,64,1024]{2,1,0:T(8,128)(2,1)S(1)}, bf16[2,64,1024]{2,1,0:T(8,128)(2,1)}, u32[]{:S(2)}) copy-start(bf16[2,64,1024]{2,1,0:T(8,128)(2,1)} %param.20) | copy-start | bytes 786436
  73.4 13.1 %copy-start.12 = (bf16[2,256,1024]{2,1,0:T(8,128)(2,1)S(1)}, bf16[2,256,1024]{2,1,0:T(8,128)(2,1)}, u32[]{:S(2)}) copy-start(bf16[2,256,1024]{2,1,0:T(8,128)(2,1)} %param.24) | copy-start | bytes 3145732
  114.3 0.7 copy-start.7
  114.3 0.7 copy-start.8
  114.4 498.9 %all-reduce.5.cloned.1.call-start = ((), (), s32[]{:S(2)}) async-start(), calls=%async_computation.1 | async-start | bytes 33554432 | tf_op jit(solution)/shard_map/psum | solution.py:50
  327.1 6.2 copy-start.1
  339.0 6.6 %copy-start.3 = (bf16[8192,1024]{1,0:T(8,128)(2,1)}, bf16[8192,1024]{1,0:T(8,128)(2,1)S(1)}, u32[]{:S(2)}) copy-start(bf16[8192,1024]{1,0:T(8,128)(2,1)S(1)} %fusion.6) | copy-start | bytes 50331652
  378.4 13.1 %copy-start.11 = (f32[1,256]{1,0:T(1,128)S(1)}, f32[1,256]{1,0:T(1,128)}, u32[]{:S(2)}) copy-start(f32[1,256]{1,0:T(1,128)} %get-tuple-element.13) | copy-start | bytes 3076
  378.4 13.1 %copy-start.13 = (bf16[2,256,1024]{2,1,0:T(8,128)(2,1)S(1)}, bf16[2,256,1024]{2,1,0:T(8,128)(2,1)}, u32[]{:S(2)}) copy-start(bf16[2,256,1024]{2,1,0:T(8,128)(2,1)} %param.24) | copy-start | bytes 3145732
  378.4 13.1 %copy-start.14 = (bf16[2,1024,256]{2,1,0:T(8,128)(2,1)S(1)}, bf16[2,1024,256]{2,1,0:T(8,128)(2,1)}, u32[]{:S(2)}) copy-start(bf16[2,1024,256]{2,1,0:T(8,128)(2,1)} %param.22) | copy-start | bytes 3145732
Sparse Core Ops, SparseCore 0:
  114.5 196.9 all-reduce.2
  421.7 191.5 all-reduce.4
where the time goes:
time: 650 us; the launch traced here: 640 us
  waiting for transfers between devices  388 us (60%)
  matrix products  149 us (23%)
  other arithmetic  82.1 us (13%)
  between operations  14.2 us (2%)
    psum x2, waiting for transfers between devices, per_device(): reduced = lax.psum(part_sum.astype(jnp.bfloat16), 'tp')  388 us
    dot_general x2, matrix products, local_branches(): jnp.dot(activated, w_down, preferred_element_type=jnp.float32)  57.7 us
    dot_general x4, matrix products, project(): projected = jnp.dot(normed, weight, preferred_element_type=jnp.float32)  30.7 us
    dot_general x2, matrix products, local_branches(): jnp.einsum('bhqk,bkhd->bqhd', attn_prob, values_all, preferred_element_ty...  28.2 us
    dot_general x2, matrix products, local_branches(): attn_part = jnp.dot(mixed_val, w_out, preferred_element_type=jnp.float32)  26.2 us
    reduce_sum x2, other arithmetic, layer_norm(): mean_val = jnp.mean(values, axis=-1, keepdims=True)  22.6 us
    convert_element_type x1, other arithmetic, per_device(): current = summed.astype(jnp.bfloat16).reshape(n_images, seq_len, model_dim)  19.5 us
    reduce_sum x6, other arithmetic, layer_norm(): variance = jnp.mean(centered * centered, axis=-1, keepdims=True)  17 us
  transfers between devices with their start and end apart: 2, of which 2 were waited for; matrix products, arithmetic and copies ran while one was open for 0% of the time, Pallas kernels for 0%

commit v1 on v0

v1 whole, which is shorter than its diff:
```python
import functools

import jax
import jax.numpy as jnp
from jax import lax
from jax.experimental import pallas as pl
from jax.experimental.pallas import tpu as pltpu
from jax.sharding import PartitionSpec as P

LN_EPS = 1e-6
LOG2E = 1.4426950408889634
VMEM_BYTES = 48 * 1024 * 1024


def norm_rows(values, scale_row):
    mean_val = jnp.mean(values, axis=-1, keepdims=True)
    centered = values - mean_val
    variance = jnp.mean(centered * centered, axis=-1, keepdims=True)
    return (centered * lax.rsqrt(variance + LN_EPS) * scale_row).astype(jnp.bfloat16)


def norm_cols(values, scale_col):
    mean_val = jnp.mean(values, axis=0, keepdims=True)
    centered = values - mean_val
    variance = jnp.mean(centered * centered, axis=0, keepdims=True)
    return (centered * lax.rsqrt(variance + LN_EPS) * scale_col).astype(jnp.bfloat16)


def branches(normed, w_ref, b_up, q_col, k_col, seq_len, head_dim):
    tokens = normed.shape[0]
    mlp = b_up.shape[1]
    qkv = 3 * head_dim
    up_end = qkv + mlp
    proj = lax.dot_general(w_ref[0:qkv], normed, (((1,), (1,)), ((), ())), preferred_element_type=jnp.float32)
    queries = norm_cols(proj[0:head_dim], q_col)
    keys_all = norm_cols(proj[head_dim : 2 * head_dim], k_col)
    values_all = proj[2 * head_dim : qkv].astype(jnp.bfloat16)
    pre_act = lax.dot_general(normed, w_ref[qkv:up_end], (((1,), (1,)), ((), ())), preferred_element_type=jnp.float32)
    activated = jax.nn.gelu(pre_act + b_up, approximate=True).astype(jnp.bfloat16)
    mixed = []
    for img in range(tokens // seq_len):
        cols = slice(img * seq_len, (img + 1) * seq_len)
        scores = lax.dot_general(keys_all[:, cols], queries[:, cols], (((0,), (0,)), ((), ())), preferred_element_type=jnp.float32)
        top = jnp.max(scores, axis=0, keepdims=True)
        expd = jnp.exp2((scores - top) * (LOG2E * head_dim**-0.5))
        prob = (expd * (1.0 / jnp.sum(expd, axis=0, keepdims=True))).astype(jnp.bfloat16)
        mixed.append(jnp.dot(values_all[:, cols], prob, preferred_element_type=jnp.float32))
    mixed_rows = jnp.concatenate(mixed, axis=1).T.astype(jnp.bfloat16)
    both = jnp.concatenate([activated, mixed_rows], axis=1)
    return jnp.dot(both, w_ref[up_end:], preferred_element_type=jnp.float32)


def first_kernel(seq_len, head_dim, x_ref, w_ref, ln_ref, b_ref, q_ref, k_ref, out_ref):
    normed = norm_rows(x_ref[...].astype(jnp.float32), ln_ref[...])
    out_ref[...] = branches(normed, w_ref, b_ref[...], q_ref[...], k_ref[...], seq_len, head_dim).astype(out_ref.dtype)


def second_kernel(seq_len, head_dim, x_ref, r_ref, bias0_ref, bias1_ref, w_ref, ln_ref, b_ref, q_ref, k_ref, out_ref, h_ref, acc_ref):
    step = pl.program_id(0)

    @pl.when(step == 0)
    def _():
        start = (x_ref[...].astype(jnp.float32) + bias0_ref[...] + r_ref[...].astype(jnp.float32)).astype(jnp.bfloat16).astype(jnp.float32)
        h_ref[...] = norm_rows(start, ln_ref[...])
        acc_ref[...] = start + bias1_ref[...]

    acc_ref[...] += branches(h_ref[...], w_ref.at[0], b_ref[0], q_ref[...], k_ref[...], seq_len, head_dim)

    @pl.when(step == pl.num_programs(0) - 1)
    def _():
        out_ref[...] = acc_ref[...].astype(out_ref.dtype)


def solution(mesh):
    col_spec = P(None, None, "tp")
    row_spec = P(None, "tp", None)
    in_specs = (P("dp", None, None), P(), col_spec, col_spec, col_spec, P(), P(), row_spec, P(), col_spec, P(None, "tp"), row_spec, P())
    tp = mesh.shape["tp"]
    dp = mesh.shape["dp"]

    def per_device(tokens_in, ln_scale, w_query, w_key, w_value, q_scale, k_scale, w_out, b_out, w_up, b_up, w_down, b_down):
        n_images, seq_len, model_dim = tokens_in.shape
        n_tokens = n_images * seq_len
        head_dim = q_scale.shape[1]
        mlp = w_up.shape[2]
        share = n_tokens // tp
        tokens = tokens_in.reshape(n_tokens, model_dim)
        f32 = jnp.float32

        def packed(layer):
            return jnp.concatenate([w_query[layer].T, w_key[layer].T, w_value[layer].T, w_up[layer].T, w_down[layer], w_out[layer]], axis=0)

        pack0, pack1 = packed(0), packed(1)
        rows = pack1.shape[0]
        piece = rows // dp
        mine = lax.dynamic_slice_in_dim(pack1, lax.axis_index("dp") * piece, piece, 0)
        gathered = lax.all_gather(mine, ("tp", "dp"), axis=0, tiled=True).reshape(tp, rows, model_dim)
        b_up_all = lax.all_gather(b_up[1:2].astype(f32), "tp", axis=0).reshape(tp, 1, mlp)
        bias = (b_out.astype(f32) + b_down.astype(f32)).reshape(-1, 1, model_dim)
        ln_rows = ln_scale.astype(f32).reshape(-1, 1, model_dim)
        q_cols = q_scale.astype(f32).reshape(-1, head_dim, 1)
        k_cols = k_scale.astype(f32).reshape(-1, head_dim, 1)

        def whole(shape):
            return pl.BlockSpec(shape, lambda i: (0,) * len(shape))

        flops = 2 * n_tokens * model_dim * (rows + seq_len // 2)
        part = pl.pallas_call(
            functools.partial(first_kernel, seq_len, head_dim),
            grid=(tp,),
            out_shape=jax.ShapeDtypeStruct((n_tokens, model_dim), jnp.bfloat16),
            in_specs=[
                pl.BlockSpec((share, model_dim), lambda i: (i, 0)),
                whole((rows, model_dim)), whole((1, model_dim)), whole((1, mlp)), whole((head_dim, 1)), whole((head_dim, 1)),
            ],
            out_specs=pl.BlockSpec((share, model_dim), lambda i: (i, 0)),
            compiler_params=pltpu.CompilerParams(vmem_limit_bytes=VMEM_BYTES),
            cost_estimate=pl.CostEstimate(flops=flops, bytes_accessed=4 * n_tokens * model_dim, transcendentals=0),
            name="first_layer",
        )(tokens, pack0, ln_rows[0], b_up[0:1].astype(f32), q_cols[0], k_cols[0])
        reduced = lax.psum_scatter(part, "tp", scatter_dimension=0, tiled=True)
        own = lax.dynamic_slice_in_dim(tokens, lax.axis_index("tp") * share, share, 0)
        out = pl.pallas_call(
            functools.partial(second_kernel, seq_len, head_dim),
            grid=(tp,),
            out_shape=jax.ShapeDtypeStruct((share, model_dim), jnp.bfloat16),
            in_specs=[
                whole((share, model_dim)), whole((share, model_dim)), whole((1, model_dim)), whole((1, model_dim)),
                pl.BlockSpec((1, rows, model_dim), lambda i: (i, 0, 0)),
                whole((1, model_dim)), pl.BlockSpec((1, 1, mlp), lambda i: (i, 0, 0)), whole((head_dim, 1)), whole((head_dim, 1)),
            ],
            out_specs=whole((share, model_dim)),
            scratch_shapes=[pltpu.VMEM((share, model_dim), jnp.bfloat16), pltpu.VMEM((share, model_dim), f32)],
            compiler_params=pltpu.CompilerParams(vmem_limit_bytes=VMEM_BYTES),
            cost_estimate=pl.CostEstimate(flops=flops, bytes_accessed=2 * tp * rows * model_dim, transcendentals=0),
            name="second_layer",
        )(own, reduced, bias[0], bias[1], gathered, ln_rows[1], b_up_all, q_cols[1], k_cols[1])
        encoded = lax.all_gather(out, "tp", axis=0, tiled=True)
        return encoded.reshape(n_images, seq_len, model_dim)

    return jax.shard_map(per_device, mesh=mesh, in_specs=in_specs, out_specs=P("dp", None, None), check_vma=False)
```

time: 650 us -> 437 us (0.67); the launches traced: 640 us -> 437 us
  matrix products: 149 us -> 0 us
  waiting for transfers between devices: 388 us -> 289 us
  Pallas kernels: 0 us -> 83 us
  other arithmetic: 82.1 us -> 0.02 us
  blocking collectives: 0 us -> 22.8 us
  local copies, waits for them, and re-layouts: 5.89 us -> 27 us
    psum x2 -> x0, waiting for transfers between devices: 388 us -> none  [per_device(): reduced = lax.psum(part_sum.astype(jnp.bfloat16), 'tp')]
    all_gather x0 -> x2, waiting for transfers between devices: none -> 192 us  [the longest x1 102 us: per_device(): lax.all_gather(mine, ('tp', 'dp'), axis=0, tiled=True)]
    dot_general x12 -> x0, matrix products: 149 us -> none  [the longest x2 57.7 us: local_branches(): jnp.dot(activated, w_down, preferred_element_type=jnp.float32)]
    reduce_scatter x0 -> x1, waiting for transfers between devices: none -> 96.9 us  [per_device(): reduced = lax.psum_scatter(part, 'tp', scatter_dimension=0, tiled=True)]
    pallas_call x0 -> x2, Pallas kernels: none -> 83 us  [the longest x1 43.8 us: per_device(): pl.pallas_call(functools.partial(first_kernel, seq_len, head_dim), grid=(...]
    reduce_sum x8 -> x0, other arithmetic: 39.7 us -> none  [the longest x2 22.6 us: layer_norm(): mean_val = jnp.mean(values, axis=-1, keepdims=True)]
    convert_element_type x4 -> x2, other arithmetic: 30.9 us -> 0.01 us  [the longest x1 0.01 us: per_device(): q_cols = q_scale.astype(f32).reshape(-1, head_dim, 1)]
    all_gather x0 -> x1, blocking collectives: none -> 22.8 us  [per_device(): lax.all_gather(b_up[1:2].astype(f32), 'tp', axis=0).reshape(tp, 1, mlp)]
  transfers between devices with their start and end apart: 2 -> 3, of which waited for: 2 -> 3; matrix products, arithmetic and copies ran while one was open for 0% -> 1% of each run, Pallas kernels for 0% -> 0%
where the time goes in v1:
time: 437 us
  waiting for transfers between devices  289 us (66%)
  Pallas kernels  83 us (19%)
  local copies, waits for them, and re-layouts  27 us (6%)
  blocking collectives  22.8 us (5%)
  between operations  15.1 us (3%)
    all_gather x1, waiting for transfers between devices, per_device(): lax.all_gather(mine, ('tp', 'dp'), axis=0, tiled=True)  102 us
    reduce_scatter x1, waiting for transfers between devices, per_device(): reduced = lax.psum_scatter(part, 'tp', scatter_dimension=0, tiled=True)  96.9 us
    all_gather x1, waiting for transfers between devices, per_device(): encoded = lax.all_gather(out, 'tp', axis=0, tiled=True)  89.8 us
    pallas_call x1, Pallas kernels, per_device(): pl.pallas_call(functools.partial(first_kernel, seq_len, head_dim), grid=(...  43.8 us
    pallas_call x1, Pallas kernels, per_device(): pl.pallas_call(functools.partial(second_kernel, seq_len, head_dim), grid=...  39.1 us
    all_gather x1, blocking collectives, per_device(): lax.all_gather(b_up[1:2].astype(f32), 'tp', axis=0).reshape(tp, 1, mlp)  22.8 us
    unnamed x28, local copies, waits for them, and re-layouts  21.6 us
  transfers between devices with their start and end apart: 3, of which 3 were waited for; matrix products, arithmetic and copies ran while one was open for 1% of the time, Pallas kernels for 0%

profile of v1, /device:TPU:21, one launch (start us, length us, event | category | flops | bytes accessed | tf_op | source)
XLA Modules:
  0.0 436.8 jit_solution(15262139182071982237)
XLA Ops:
  7.4 0.0 reduce-scatter.2.cloned.1.call-start
  7.4 1.7 bitcast_dynamic-update-slice_fusion.6
  9.1 1.3 fusion
  10.3 0.0 copy-start.4
  10.3 0.0 copy-start.5
  10.4 0.0 copy-start.8
  10.4 0.0 copy-start.9
  10.4 0.0 copy-start.2
  10.4 0.2 copy.27
  10.6 0.2 copy.26
  10.8 0.2 copy-done.4
  11.0 0.0 copy-done.5
  11.0 0.0 copy-done.8
  11.1 0.1 copy.21.q_ref
  11.2 0.0 copy-done.9
  11.2 0.1 copy.22.k_ref
  11.3 0.1 copy-done.2
  11.3 0.0 copy-start.1
  11.3 0.7 bitcast_dynamic-update-slice_fusion.5
  12.0 1.6 bitcast_dynamic-update-slice_fusion.4
  13.7 0.9 bitcast_dynamic-update-slice_fusion
  14.5 0.0 copy-start.3
  14.5 0.0 copy-done.1
  14.5 0.9 bitcast_dynamic-update-slice_fusion.2
  15.4 0.1 copy-done.3
  15.5 0.7 bitcast_dynamic-update-slice_fusion.10
  16.1 43.8 %first_layer.1 = bf16[8192,1024]{1,0:T(8,128)(2,1)} custom-call(bf16[8192,1024]{1,0:T(8,128)(2,1)} %bitcast.55, bf16[768,1024]{1,0:T(8,128)(2,1)S(1)} %get-tuple-element.10.w_ref, f32[1,1024]{1,0:T(1,128)S(1)} %get-tuple-element.20.ln_ref, f32[1,256]{1,0:T(1,128)S(1)} %get-tuple-element.26.b_ref, f32[64,1]{1,0:T(8,128)S(1)} %copy.21.q_ref, ...), custom_call_target="tpu_custom_call" | custom-call | flops 15032385536 | bytes 33554432 | tf_op jit(solution)/shard_map/first_layer/pallas_call | solution.py:108
  60.0 0.1 reduce-scatter.2.cloned.1.call-update
  60.0 0.1 all-gather.5.cloned.1.call-start
  60.1 0.0 copy-start.6
  60.1 0.0 copy-start.7
  60.1 1.8 constant_dynamic-slice_fusion
  61.9 0.1 all-gather.5.cloned.1.call-update
  62.0 0.1 all-gather.7.cloned.1.call-start
  62.0 0.1 copy.24.q_ref
  62.1 0.1 copy.25.k_ref
  62.2 22.8 %all-gather.1.b_ref = f32[16,1,256]{2,1,0:T(1,128)S(1)} all-gather(f32[1,1,256]{2,1,0:T(1,128)S(1)} %get-tuple-element.25), channel_id=2, replica_groups=mesh['dp'=4,'tp'=16] {'tp'}, dimensions={0}, use_global_device_ids=true | all-gather | bytes 17408 | tf_op jit(solution)/shard_map/all_gather | solution.py:98
  85.0 1.3 constant_dynamic-slice_fusion.1.x_ref
  86.3 0.0 copy-done.6
  86.3 0.0 copy-done.7
  86.4 96.9 %reduce-scatter.2.cloned.1.call-done.r_ref = bf16[512,1024]{1,0:T(8,128)(2,1)} async-done(((bf16[8192,1024]{1,0:T(8,128)(2,1)}), bf16[512,1024]{1,0:T(8,128)(2,1)}) %reduce-scatter.2.cloned.1.call-update) | async-done | bytes 1048592 | tf_op jit(solution)/shard_map/reduce_scatter | solution.py:121
  183.3 101.9 %all-gather.5.cloned.1.call-done = bf16[12288,1024]{1,0:T(8,128)(2,1)} async-done(((bf16[192,1024]{1,0:T(8,128)(2,1)}), bf16[12288,1024]{1,0:T(8,128)(2,1)}) %all-gather.5.cloned.1.call-update) | async-done | bytes 25165840 | tf_op jit(solution)/shard_map/all_gather | solution.py:97
  285.2 0.0 copy-start
  285.2 1.2 copy-done
  286.4 39.1 %second_layer.1 = bf16[512,1024]{1,0:T(8,128)(2,1)} custom-call(bf16[512,1024]{1,0:T(8,128)(2,1)S(1)} %constant_dynamic-slice_fusion.1.x_ref, bf16[512,1024]{1,0:T(8,128)(2,1)S(1)} %copy-done, f32[1,1024]{1,0:T(1,128)S(1)} %get-tuple-element.18.bias0_ref, f32[1,1024]{1,0:T(1,128)S(1)} %get-tuple-element.17.bias1_ref, bf16[16,768,1024]{2,1,0:T(8,128)(2,1)} %bitcast.57, ...), custom_call_target="tpu_custom_call" | custom-call | flops 15032385536 | bytes 25165824 | tf_op jit(solution)/shard_map/second_layer/pallas_call | solution.py:123
  325.6 0.1 all-gather.7.cloned.1.call-update
  325.6 89.8 %all-gather.7.cloned.1.call-done = bf16[8192,1024]{1,0:T(8,128)(2,1)} async-done(((bf16[512,1024]{1,0:T(8,128)(2,1)}), bf16[8192,1024]{1,0:T(8,128)(2,1)}) %all-gather.7.cloned.1.call-update) | async-done | bytes 16777232 | tf_op jit(solution)/shard_map/all_gather | solution.py:138
  415.4 13.9 %copy.39 = bf16[32,256,1024]{2,1,0:T(8,128)(2,1)} copy(bf16[32,256,1024]{2,1,0:T(8,128)(2,1)} %bitcast.54) | data formatting | bytes 33554432
  (8 shorter events, 0.0 us)
Async XLA Ops:
  7.4 175.9 %reduce-scatter.2.cloned.1.call-start = ((), (), s32[]{:S(2)}) async-start(), calls=%async_computation.1 | async-start | bytes 17825792 | tf_op jit(solution)/shard_map/reduce_scatter | solution.py:121
  10.3 0.7 copy-start.4
  10.3 0.7 copy-start.5
  10.4 0.7 copy-start.8
  10.4 0.8 copy-start.9
  10.4 1.0 copy-start.2
  11.3 3.2 copy-start.1
  14.5 0.9 copy-start.3
  60.0 225.2 %all-gather.5.cloned.1.call-start = ((), (), s32[]{:S(2)}) async-start(), calls=%async_computation.2 | async-start | bytes 25559040 | tf_op jit(solution)/shard_map/all_gather | solution.py:97
  60.1 26.2 %copy-start.6 = (bf16[2,1024]{1,0:T(2,128)(2,1)S(1)}, bf16[2,1024]{1,0:T(2,128)(2,1)}, u32[]{:S(2)}) copy-start(bf16[2,1024]{1,0:T(2,128)(2,1)} %param.25) | copy-start | bytes 12292
  60.1 26.2 %copy-start.7 = (bf16[2,1024]{1,0:T(2,128)(2,1)S(1)}, bf16[2,1024]{1,0:T(2,128)(2,1)}, u32[]{:S(2)}) copy-start(bf16[2,1024]{1,0:T(2,128)(2,1)} %param.21) | copy-start | bytes 12292
  62.0 353.5 %all-gather.7.cloned.1.call-start = ((), (), s32[]{:S(2)}) async-start(), calls=%async_computation.3 | async-start | bytes 17825792 | tf_op jit(solution)/shard_map/all_gather | solution.py:138
  285.2 1.2 copy-start
Sparse Core Ops, SparseCore 0:
  60.1 123.0 reduce-scatter.1
  325.8 89.6 all-gather.6
Sparse Core Ops, SparseCore 1:
  63.8 221.3 all-gather.4

commit v2 on v1

v2 whole, which is shorter than its diff:
```python
import functools

import jax
import jax.numpy as jnp
from jax import lax
from jax.experimental import pallas as pl
from jax.experimental.pallas import tpu as pltpu
from jax.sharding import PartitionSpec as P

LN_EPS = 1e-6
LOG2E = 1.4426950408889634
VMEM_BYTES = 44 * 1024 * 1024
MESH = pl.DeviceIdType.MESH


def norm_rows(values, scale_row):
    mean_val = jnp.mean(values, axis=-1, keepdims=True)
    centered = values - mean_val
    variance = jnp.mean(centered * centered, axis=-1, keepdims=True)
    return (centered * lax.rsqrt(variance + LN_EPS) * scale_row).astype(jnp.bfloat16)


def norm_cols(values, scale_col):
    mean_val = jnp.mean(values, axis=0, keepdims=True)
    centered = values - mean_val
    variance = jnp.mean(centered * centered, axis=0, keepdims=True)
    return (centered * lax.rsqrt(variance + LN_EPS) * scale_col).astype(jnp.bfloat16)


def branches(normed, w_ref, b_up, q_col, k_col, seq_len, head_dim):
    tokens = normed.shape[0]
    mlp = b_up.shape[1]
    qkv = 3 * head_dim
    up_end = qkv + mlp
    proj = lax.dot_general(w_ref[0:qkv], normed, (((1,), (1,)), ((), ())), preferred_element_type=jnp.float32)
    queries = norm_cols(proj[0:head_dim], q_col)
    keys_all = norm_cols(proj[head_dim : 2 * head_dim], k_col)
    values_all = proj[2 * head_dim : qkv].astype(jnp.bfloat16)
    pre_act = lax.dot_general(normed, w_ref[qkv:up_end], (((1,), (1,)), ((), ())), preferred_element_type=jnp.float32)
    activated = jax.nn.gelu(pre_act + b_up, approximate=True).astype(jnp.bfloat16)
    mixed = []
    for img in range(tokens // seq_len):
        cols = slice(img * seq_len, (img + 1) * seq_len)
        scores = lax.dot_general(keys_all[:, cols], queries[:, cols], (((0,), (0,)), ((), ())), preferred_element_type=jnp.float32)
        top = jnp.max(scores, axis=0, keepdims=True)
        expd = jnp.exp2((scores - top) * (LOG2E * head_dim**-0.5))
        prob = (expd * (1.0 / jnp.sum(expd, axis=0, keepdims=True))).astype(jnp.bfloat16)
        mixed.append(jnp.dot(values_all[:, cols], prob, preferred_element_type=jnp.float32))
    mixed_rows = jnp.concatenate(mixed, axis=1).T.astype(jnp.bfloat16)
    both = jnp.concatenate([activated, mixed_rows], axis=1)
    return jnp.dot(both, w_ref[up_end:], preferred_element_type=jnp.float32)


def neighbours(tp):
    me = lax.axis_index("tp")
    chips = tp // 2
    core = lax.rem(me, 2)
    chip = me // 2
    right = lax.rem(chip + 1, chips) * 2 + core
    left = lax.rem(chip + chips - 1, chips) * 2 + core
    return core, chip, right, left, me + 1 - 2 * core


def enter(peers):
    barrier = pltpu.get_barrier_semaphore()
    for peer in peers:
        pl.semaphore_signal(barrier, inc=1, device_id={"tp": peer}, device_id_type=MESH)
    pl.semaphore_wait(barrier, len(peers))


def first_kernel(seq_len, head_dim, tp, x_hbm, w_ref, ln_ref, b_ref, q_ref, k_ref, bias_ref, y_ref, x_buf, ring, from_partner, to_partner, mine, x_sem, ring_send, ring_recv, pair_send, pair_recv):
    core, chip, right, left, partner = neighbours(tp)
    chips = tp // 2
    half = x_buf.shape[1] // 2
    sub_rows = half // 2
    items = 2 * chips
    enter((right, left, partner))

    def x_copies(item):
        way = lax.rem(item, 2)
        there = lax.rem(chip + 2 * chips + (1 + item // 2) * (2 * way - 1), chips)
        slot = lax.rem(item, 2)
        return [
            pltpu.make_async_copy(
                x_hbm.at[pl.ds(pl.multiple_of((2 * there + owner) * (2 * half) + way * half, half), half)],
                x_buf.at[slot, pl.ds(place * half, half)],
                x_sem.at[slot, place],
            )
            for place, owner in ((0, 1 - core), (1, core))
        ]

    def pair_copy(item):
        return pltpu.make_async_remote_copy(
            src_ref=to_partner.at[item], dst_ref=from_partner.at[item],
            send_sem=pair_send.at[item], recv_sem=pair_recv.at[item],
            device_id={"tp": partner}, device_id_type=MESH,
        )

    def ring_copy(step, way, sub):
        return pltpu.make_async_remote_copy(
            src_ref=ring.at[step, way, sub], dst_ref=ring.at[step + 1, way, sub],
            send_sem=ring_send.at[step, way, sub], recv_sem=ring_recv.at[step, way, sub],
            device_id={"tp": left if way else right}, device_id_type=MESH,
        )

    for copy in x_copies(0):
        copy.start()

    def turn(index, carry):
        t = index - 2

        @pl.when(t >= 0)
        def _():
            step = t // 2
            sub = lax.rem(t, 2)
            rows = pl.ds(pl.multiple_of(sub * sub_rows, sub_rows), sub_rows)
            for way in range(2):
                item = 2 * step + way

                @pl.when(sub == 0)
                def _():
                    pair_copy(item).wait_recv()

                local = from_partner[item, rows].astype(jnp.float32) + mine[lax.rem(item, 4), rows].astype(jnp.float32)

                @pl.when(step == 0)
                def _():
                    ring[0, way, sub] = local.astype(ring.dtype)

                @pl.when(step > 0)
                def _():
                    ring_copy(step - 1, way, sub).wait_recv()

                @pl.when(jnp.logical_and(step > 0, step < chips - 1))
                def _():
                    ring[step, way, sub] = (ring[step, way, sub].astype(jnp.float32) + local).astype(ring.dtype)

                @pl.when(step < chips - 1)
                def _():
                    ring_copy(step, way, sub).start()

                @pl.when(step == chips - 1)
                def _():
                    own = x_buf[way, pl.ds(pl.multiple_of(half + sub * sub_rows, sub_rows), sub_rows)].astype(jnp.float32)
                    total = ring[chips - 1, way, sub].astype(jnp.float32) + local
                    y_ref[pl.ds(pl.multiple_of(way * half + sub * sub_rows, sub_rows), sub_rows)] = (own + bias_ref[...] + total).astype(y_ref.dtype)

        @pl.when(index < items)
        def _():
            @pl.when(index + 1 < items)
            def _():
                for copy in x_copies(index + 1):
                    copy.start()

            for copy in x_copies(index):
                copy.wait()
            normed = norm_rows(x_buf[lax.rem(index, 2)].astype(jnp.float32), ln_ref[...])
            part = branches(normed, w_ref, b_ref[...], q_ref[...], k_ref[...], seq_len, head_dim).astype(jnp.bfloat16)
            to_partner[index] = part[:half]
            mine[lax.rem(index, 4)] = part[half:]
            pair_copy(index).start()

        return carry

    lax.fori_loop(0, items + 2, turn, 0)

    def drain(item, carry):
        pair_copy(item).wait_send()
        return carry

    lax.fori_loop(0, items, drain, 0)

    def drain_ring(step, carry):
        for way in range(2):
            for sub in range(2):
                ring_copy(step, way, sub).wait_send()
        return carry

    lax.fori_loop(0, chips - 1, drain_ring, 0)


def second_kernel(seq_len, head_dim, tp, dp, y_ref, w_hbm, ln_ref, bias_ref, q_ref, k_ref, out_ref, w_buf, h_ref, acc_ref, w_sem, ring_send, ring_recv, pair_send, pair_recv):
    core, chip, right, left, partner = neighbours(tp)
    chips = tp // 2
    share = y_ref.shape[0]
    images = share // seq_len
    rows = w_buf.shape[1] - 8
    piece = rows // dp
    sub_rows = seq_len // 4
    mlp = rows - 4 * head_dim - (rows - 4 * head_dim) // 2
    enter((right, left, partner))

    def w_copies(turn):
        shard = lax.rem(turn, tp)
        slot = lax.rem(turn, 2)
        copies = []
        for part in range(dp):
            base = (shard * dp + part) * (piece + 8)
            copies.append((pl.multiple_of(base, 8), piece, part * piece, part))
        copies.append((pl.multiple_of(shard * dp * (piece + 8) + piece, 8), 8, rows, dp))
        return [pltpu.make_async_copy(w_hbm.at[pl.ds(src, n)], w_buf.at[slot, pl.ds(dst, n)], w_sem.at[slot, place]) for src, n, dst, place in copies]

    def chunk(image, way, sub, owner):
        offset = owner * share + image * seq_len + way * (2 * sub_rows) + sub * sub_rows
        return out_ref.at[pl.ds(pl.multiple_of(offset, sub_rows), sub_rows)]

    def origin(way, step):
        back = chip - step if way == 0 else chip + step
        return 2 * lax.rem(back + chips, chips)

    def ring_copy(image, way, sub, step):
        ref = chunk(image, way, sub, origin(way, step) + core)
        return pltpu.make_async_remote_copy(
            src_ref=ref, dst_ref=ref, send_sem=ring_send.at[image, way, sub, step], recv_sem=ring_recv.at[image, way, sub, step],
            device_id={"tp": left if way else right}, device_id_type=MESH,
        )

    def arrival(image, way, sub, step):
        ref = chunk(image, way, sub, origin(way, step + 1) + core)
        return pltpu.make_async_remote_copy(
            src_ref=ref, dst_ref=ref, send_sem=ring_send.at[image, way, sub, step], recv_sem=ring_recv.at[image, way, sub, step],
            device_id={"tp": left if way else right}, device_id_type=MESH,
        )

    def pair_copy(image, way, sub, step, who):
        ref = chunk(image, way, sub, origin(way, step) + who)
        return pltpu.make_async_remote_copy(
            src_ref=ref, dst_ref=ref, send_sem=pair_send.at[image, way, sub, step], recv_sem=pair_recv.at[image, way, sub, step],
            device_id={"tp": partner}, device_id_type=MESH,
        )

    def event(image, number):
        step = number // 2
        sub = lax.rem(number, 2)
        for way in range(2):
            arrival(image, way, sub, step).wait_recv()

            @pl.when(step + 1 < chips - 1)
            def _():
                ring_copy(image, way, sub, step + 1).start()

            pair_copy(image, way, sub, step + 1, core).start()

    for copy in w_copies(0):
        copy.start()
    start = y_ref[...].astype(jnp.float32)
    h_ref[...] = norm_rows(start, ln_ref[...])
    acc_ref[...] = start + bias_ref[...]

    def turn(index, carry):
        image = index // tp
        shard = lax.rem(index, tp)

        @pl.when(index + 1 < images * tp)
        def _():
            for copy in w_copies(index + 1):
                copy.start()

        @pl.when(jnp.logical_and(image > 0, lax.rem(shard, 2) == 0))
        def _():
            event(image - 1, shard // 2)

        for copy in w_copies(index):
            copy.wait()
        slot = lax.rem(index, 2)
        span = pl.ds(pl.multiple_of(image * seq_len, seq_len), seq_len)
        b_up = w_buf[slot, pl.ds(rows, 8)].astype(jnp.float32)[0:1, 0:mlp]
        acc_ref[span] += branches(h_ref[span], w_buf.at[slot, pl.ds(0, rows)], b_up, q_ref[...], k_ref[...], seq_len, head_dim)

        @pl.when(shard == tp - 1)
        def _():
            me = 2 * chip + core
            out_ref[pl.ds(pl.multiple_of(me * share + image * seq_len, seq_len), seq_len)] = acc_ref[span].astype(out_ref.dtype)
            for sub in range(2):
                for way in range(2):
                    ring_copy(image, way, sub, 0).start()
            for sub in range(2):
                for way in range(2):
                    pair_copy(image, way, sub, 0, core).start()

        return carry

    lax.fori_loop(0, images * tp, turn, 0)
    total = 2 * (chips - 1)
    done = tp // 2

    def tail(number, carry):
        @pl.when(number + done < total)
        def _():
            event(images - 2, number + done)

        event(images - 1, number)
        return carry

    lax.fori_loop(0, total, tail, 0)

    def drain(step, carry):
        for image in range(images):
            for way in range(2):
                for sub in range(2):
                    @pl.when(step < chips - 1)
                    def _():
                        ring_copy(image, way, sub, step).wait_send()

                    pair_copy(image, way, sub, step, core).wait_send()
                    pair_copy(image, way, sub, step, 1 - core).wait_recv()
        return carry

    lax.fori_loop(0, chips, drain, 0)


def solution(mesh):
    col_spec = P(None, None, "tp")
    row_spec = P(None, "tp", None)
    in_specs = (P("dp", None, None), P(), col_spec, col_spec, col_spec, P(), P(), row_spec, P(), col_spec, P(None, "tp"), row_spec, P())
    tp = mesh.shape["tp"]
    dp = mesh.shape["dp"]
    chips = tp // 2

    def per_device(tokens_in, ln_scale, w_query, w_key, w_value, q_scale, k_scale, w_out, b_out, w_up, b_up, w_down, b_down):
        n_images, seq_len, model_dim = tokens_in.shape
        n_tokens = n_images * seq_len
        head_dim = q_scale.shape[1]
        mlp = w_up.shape[2]
        share = n_tokens // tp
        half = share // 2
        images = share // seq_len
        tokens = tokens_in.reshape(n_tokens, model_dim)
        f32, bf16 = jnp.float32, jnp.bfloat16

        def packed(layer):
            return jnp.concatenate([w_query[layer].T, w_key[layer].T, w_value[layer].T, w_up[layer].T, w_down[layer], w_out[layer]], axis=0)

        pack0, pack1 = packed(0), packed(1)
        rows = pack1.shape[0]
        piece = rows // dp
        bias_rows = jnp.pad(b_up[1:2], ((0, 7), (0, model_dim - mlp)))
        mine = jnp.concatenate([lax.dynamic_slice_in_dim(pack1, lax.axis_index("dp") * piece, piece, 0), bias_rows], axis=0)
        pack0, mine = lax.optimization_barrier((pack0, mine))
        gathered = lax.all_gather(mine, ("tp", "dp"), axis=0, tiled=True)
        bias = (b_out.astype(f32) + b_down.astype(f32)).reshape(-1, 1, model_dim)
        ln_rows = ln_scale.astype(f32).reshape(-1, 1, model_dim)
        q_cols = q_scale.astype(f32).reshape(-1, head_dim, 1)
        k_cols = k_scale.astype(f32).reshape(-1, head_dim, 1)
        vmem = pl.BlockSpec(memory_space=pltpu.VMEM)
        hbm = pl.BlockSpec(memory_space=pl.ANY)
        dma = pltpu.SemaphoreType.DMA
        flops = 2 * n_tokens * model_dim * (rows + seq_len // 2)
        middle = pl.pallas_call(
            functools.partial(first_kernel, seq_len, head_dim, tp),
            out_shape=jax.ShapeDtypeStruct((share, model_dim), bf16),
            in_specs=[hbm] + [vmem] * 6,
            out_specs=vmem,
            scratch_shapes=[
                pltpu.VMEM((2, share, model_dim), bf16),
                pltpu.VMEM((chips, 2, 2, half // 2, model_dim), bf16),
                pltpu.VMEM((tp, half, model_dim), bf16),
                pltpu.VMEM((tp, half, model_dim), bf16),
                pltpu.VMEM((4, half, model_dim), bf16),
                dma((2, 2)), dma((chips - 1, 2, 2)), dma((chips - 1, 2, 2)), dma((tp,)), dma((tp,)),
            ],
            compiler_params=pltpu.CompilerParams(vmem_limit_bytes=VMEM_BYTES, collective_id=0, has_side_effects=True),
            cost_estimate=pl.CostEstimate(flops=4 * flops, bytes_accessed=4 * n_tokens * model_dim, transcendentals=0),
            name="first_layer",
        )(tokens, pack0, ln_rows[0], b_up[0:1].astype(f32), q_cols[0], k_cols[0], bias[0])
        out = pl.pallas_call(
            functools.partial(second_kernel, seq_len, head_dim, tp, dp),
            out_shape=jax.ShapeDtypeStruct((n_tokens, model_dim), bf16),
            in_specs=[vmem, hbm] + [vmem] * 4,
            out_specs=vmem,
            scratch_shapes=[
                pltpu.VMEM((2, rows + 8, model_dim), bf16),
                pltpu.VMEM((share, model_dim), bf16), pltpu.VMEM((share, model_dim), f32),
                dma((2, dp + 1)), dma((images, 2, 2, chips)), dma((images, 2, 2, chips)), dma((images, 2, 2, chips)), dma((images, 2, 2, chips)),
            ],
            compiler_params=pltpu.CompilerParams(vmem_limit_bytes=VMEM_BYTES, collective_id=1, has_side_effects=True),
            cost_estimate=pl.CostEstimate(flops=4 * flops, bytes_accessed=2 * tp * rows * model_dim, transcendentals=0),
            name="second_layer",
        )(middle, gathered, ln_rows[1], bias[1], q_cols[1], k_cols[1])
        return out.reshape(n_images, seq_len, model_dim)

    return jax.shard_map(per_device, mesh=mesh, in_specs=in_specs, out_specs=P("dp", None, None), check_vma=False)
```

time: 437 us -> 359 us (0.82)
  waiting for transfers between devices: 289 us -> 72.4 us
  Pallas kernels: 83 us -> 249 us
  blocking collectives: 22.8 us -> 0 us
  local copies, waits for them, and re-layouts: 27 us -> 22 us
    pallas_call x2, Pallas kernels: 83 us -> 249 us  [the longest x1 133 us: per_device(): pl.pallas_call(functools.partial(first_kernel, seq_len, head_dim, tp), ou...]
    all_gather x2 -> x1, waiting for transfers between devices: 192 us -> 72.4 us  [per_device(): gathered = lax.all_gather(mine, ('tp', 'dp'), axis=0, tiled=True)]
    reduce_scatter x1 -> x0, waiting for transfers between devices: 96.9 us -> none  [per_device(): reduced = lax.psum_scatter(part, 'tp', scatter_dimension=0, tiled=True)]
    all_gather x1 -> x0, blocking collectives: 22.8 us -> none  [per_device(): lax.all_gather(b_up[1:2].astype(f32), 'tp', axis=0).reshape(tp, 1, mlp)]
  transfers between devices with their start and end apart: 3 -> 1, of which waited for: 3 -> 1; matrix products, arithmetic and copies ran while one was open for 1% -> 0% of each run, Pallas kernels for 0% -> 37%
where the time goes in v2:
time: 359 us
  Pallas kernels  249 us (69%)
  waiting for transfers between devices  72.4 us (20%)
  local copies, waits for them, and re-layouts  22 us (6%)
  between operations  13.6 us (4%)
    pallas_call x1, Pallas kernels, per_device(): pl.pallas_call(functools.partial(first_kernel, seq_len, head_dim, tp), ou...  133 us
    pallas_call x1, Pallas kernels, per_device(): pl.pallas_call(functools.partial(second_kernel, seq_len, head_dim, tp, dp...  116 us
    all_gather x1, waiting for transfers between devices, per_device(): gathered = lax.all_gather(mine, ('tp', 'dp'), axis=0, tiled=True)  72.4 us
    unnamed x28, local copies, waits for them, and re-layouts  18.7 us
  transfers between devices with their start and end apart: 1, of which 1 were waited for; matrix products, arithmetic and copies ran while one was open for 0% of the time, Pallas kernels for 37%

profile of v2, /device:TPU:21, one launch (start us, length us, event | category | flops | bytes accessed | tf_op | source)
XLA Modules:
  0.0 358.6 jit_solution(9927476874780602986)
XLA Ops:
  6.5 0.0 all-gather.2.cloned.1.call-start
  6.6 0.8 slice_convert_fusion
  7.3 1.3 fusion.2
  8.6 0.0 copy-start.1
  8.6 0.0 copy-start.2
  8.6 0.0 copy-start.3
  8.6 0.2 copy.21
  8.8 0.2 copy.20
  9.0 0.5 copy-done.1
  9.5 0.7 bitcast_dynamic-update-slice_fusion.6
  10.2 0.0 copy-done.2
  10.2 0.0 copy-start
  10.2 0.7 bitcast_dynamic-update-slice_fusion.5
  10.9 0.0 copy-done.3
  10.9 0.7 bitcast_dynamic-update-slice_fusion.4
  11.6 0.9 bitcast_dynamic-update-slice_fusion
  12.4 0.0 copy-start.4
  12.4 0.0 copy-done
  12.4 0.9 bitcast_dynamic-update-slice_fusion.2
  13.3 0.0 copy-start.8
  13.3 0.0 copy-start.9
  13.3 0.0 copy-start.6
  13.3 0.0 copy-start.7
  13.3 0.0 copy-start.5
  13.3 0.1 copy-done.4
  13.4 0.7 bitcast_dynamic-update-slice_fusion.10
  14.0 1.0 constant_dynamic-slice_fusion
  15.1 0.8 fusion.1
  15.9 0.1 all-gather.2.cloned.1.call-update
  15.9 0.0 copy-done.8
  15.9 0.0 copy-done.9
  16.0 0.1 copy.19.k_ref
  16.1 0.1 copy.18.q_ref
  16.2 0.1 copy.17.k_ref
  16.3 0.1 copy.16.q_ref
  16.4 0.0 copy-done.6
  16.4 0.0 copy-done.7
  16.4 0.0 copy-done.5
  16.4 132.8 %first_layer.1.y_ref = bf16[512,1024]{1,0:T(8,128)(2,1)S(1)} custom-call(bf16[8192,1024]{1,0:T(8,128)(2,1)} %bitcast.51, bf16[768,1024]{1,0:T(8,128)(2,1)S(1)} %get-tuple-element.7.w_ref, f32[1,1024]{1,0:T(1,128)S(1)} %get-tuple-element.33.ln_ref, f32[1,256]{1,0:T(1,128)S(1)} %get-tuple-element.29.b_ref, f32[64,1]{1,0:T(8,128)S(1)} %copy.16.q_ref, ...), custom_call_target="tpu_custom_call" | custom-call | flops 60129542144 | bytes 33554432 | tf_op jit(solution)/shard_map/first_layer/pallas_call | solution.py:349
  149.2 72.4 %all-gather.2.cloned.1.call-done.w_hbm = bf16[12800,1024]{1,0:T(8,128)(2,1)} async-done(((bf16[200,1024]{1,0:T(8,128)(2,1)}), bf16[12800,1024]{1,0:T(8,128)(2,1)}) %all-gather.2.cloned.1.call-update) | async-done | bytes 26214416 | tf_op jit(solution)/shard_map/all_gather | solution.py:340
  221.6 116.2 %second_layer.1 = bf16[8192,1024]{1,0:T(8,128)(2,1)} custom-call(bf16[512,1024]{1,0:T(8,128)(2,1)S(1)} %first_layer.1.y_ref, bf16[12800,1024]{1,0:T(8,128)(2,1)} %all-gather.2.cloned.1.call-done.w_hbm, f32[1,1024]{1,0:T(1,128)S(1)} %get-tuple-element.34.ln_ref, f32[1,1024]{1,0:T(1,128)S(1)} %get-tuple-element.21.bias_ref, f32[64,1]{1,0:T(8,128)S(1)} %copy.18.q_ref, ...), custom_call_target="tpu_custom_call" | custom-call | flops 60129542144 | bytes 25165824 | tf_op jit(solution)/shard_map/second_layer/pallas_call | solution.py:366
  337.9 13.9 %copy.33 = bf16[32,256,1024]{2,1,0:T(8,128)(2,1)} copy(bf16[32,256,1024]{2,1,0:T(8,128)(2,1)} %bitcast.50) | data formatting | bytes 33554432
  (6 shorter events, 0.0 us)
Async XLA Ops:
  6.5 215.1 %all-gather.2.cloned.1.call-start = ((), (), s32[]{:S(2)}) async-start(), calls=%async_computation | async-start | bytes 26624000 | tf_op jit(solution)/shard_map/all_gather | solution.py:340
  8.6 1.0 copy-start.1
  8.6 1.6 copy-start.2
  8.6 2.3 copy-start.3
  10.2 2.2 copy-start
  12.4 0.9 copy-start.4
  13.3 2.6 copy-start.8
  13.3 2.6 copy-start.9
  13.3 3.1 copy-start.6
  13.3 3.1 copy-start.7
  13.3 3.1 copy-start.5
Sparse Core Ops, SparseCore 0:
  16.0 205.5 all-gather.1

commit v3 on v2

--- a/solution.py
+++ b/solution.py
@@ -1,4 +1,5 @@
 import functools
+import math
 
 import jax
 import jax.numpy as jnp
@@ -9,7 +10,8 @@
 
 LN_EPS = 1e-6
 LOG2E = 1.4426950408889634
-VMEM_BYTES = 44 * 1024 * 1024
+FIRST_VMEM = 46 * 1024 * 1024
+SECOND_VMEM = 24 * 1024 * 1024
 MESH = pl.DeviceIdType.MESH
 
 
@@ -63,18 +65,163 @@
 
 def enter(peers):
     barrier = pltpu.get_barrier_semaphore()
-    for peer in peers:
-        pl.semaphore_signal(barrier, inc=1, device_id={"tp": peer}, device_id_type=MESH)
+    for axis, peer in peers:
+        pl.semaphore_signal(barrier, inc=1, device_id={axis: peer}, device_id_type=MESH)
     pl.semaphore_wait(barrier, len(peers))
 
 
-def first_kernel(seq_len, head_dim, tp, x_hbm, w_ref, ln_ref, b_ref, q_ref, k_ref, bias_ref, y_ref, x_buf, ring, from_partner, to_partner, mine, x_sem, ring_send, ring_recv, pair_send, pair_recv):
+def plane_of(dp):
+    side = math.isqrt(dp)
+    return (side, side) if side * side == dp else (1, dp)
+
+
+def shard_of_round(chip, chips, number):
+    sign = 1 - 2 * (number % 2)
+    return lax.rem(chip + chips + sign * ((number + 1) // 2), chips)
+
+
+def schedule_of(chips, plane):
+    events = {}
+    for number in range(chips):
+        if number == 0:
+            events[0] = [("pass", 0, 0), ("pair", 0, 0)]
+            continue
+        begin = max(3, 2 * number)
+        events.setdefault(begin, []).append(("pass", number, 0))
+        for hop in range(1, max(plane)):
+            events.setdefault(begin + 1 + hop, []).append(("line", number, hop))
+        for hop in range(1, max(plane)):
+            events.setdefault(begin + 1 + max(plane) + hop, []).append(("plane", number, hop))
+        events.setdefault(begin + 2 * max(plane), []).append(("pair", number, 0))
+    return events
+
+
+def first_kernel(seq_len, head_dim, tp, dp, x_hbm, wq_hbm, wk_hbm, wv_hbm, wup_hbm, wdown_hbm, wout_hbm, ln_ref, b_ref, q_ref, k_ref, bo_ref, bd_ref, y_ref, w_all, b_all, pack, up_raw, x_buf, ring, from_partner, to_partner, mine, load_sem, own_sem, x_sem, ring_send, ring_recv, pair_send, pair_recv, z_send, z_recv, zb_send, zb_recv, line_send, line_recv, plane_send, plane_recv, w_send, w_recv, wb_send, wb_recv):
     core, chip, right, left, partner = neighbours(tp)
     chips = tp // 2
+    me = 2 * chip + core
+    rows = pack.shape[1]
+    mlp = up_raw.shape[2]
+    qkv = 3 * head_dim
+    plane = plane_of(dp)
+    group = lax.axis_index("dp")
+    at = (group // plane[1], lax.rem(group, plane[1]))
+    unit = rows // (2 * dp)
+
+    def group_at(axis, pos, other):
+        return pos * plane[1] + other if axis == 0 else other * plane[1] + pos
+
+    def beside(axis, sign):
+        return group_at(axis, lax.rem(at[axis] + plane[axis] + sign, plane[axis]), at[1 - axis])
+
     half = x_buf.shape[1] // 2
     sub_rows = half // 2
     items = 2 * chips
-    enter((right, left, partner))
+    peers = [("tp", right), ("tp", left), ("tp", partner)]
+    for axis in range(2):
+        peers += [("dp", beside(axis, sign)) for sign in (1, -1)[: min(plane[axis] - 1, 2)]]
+    enter(peers)
+
+    def loads(layer):
+        pieces = [(wq_hbm, pack.at[layer, 0:head_dim]), (wk_hbm, pack.at[layer, head_dim : 2 * head_dim]), (wv_hbm, pack.at[layer, 2 * head_dim : qkv]), (wup_hbm, up_raw.at[layer]), (wdown_hbm, pack.at[layer, qkv + mlp : qkv + 2 * mlp]), (wout_hbm, pack.at[layer, qkv + 2 * mlp : rows])]
+        return [pltpu.make_async_copy(src.at[layer], dst, load_sem.at[layer, place]) for place, (src, dst) in enumerate(pieces)]
+
+    def turn_up(layer):
+        for copy in loads(layer):
+            copy.wait()
+        pack[layer, qkv : qkv + mlp] = up_raw[layer].T
+
+    def block(number, start, count, owner):
+        base = (2 * shard_of_round(chip, chips, number) + owner) * rows + start
+        return w_all.at[pl.ds(pl.multiple_of(base, 8), count)]
+
+    def z_copies(number):
+        copies = []
+        for part in range(2):
+            rightwards = (part == 0) if number == chips - 1 else number % 2 == 1
+            hops = (number + 1) // 2
+            source = lax.rem(chip + chips + (1 - hops if rightwards else hops - 1), chips)
+            peer = right if rightwards else left
+            ref = w_all.at[pl.ds(pl.multiple_of((2 * source + core) * rows + (part * dp + group) * unit, 8), unit)]
+            copies.append(pltpu.make_async_remote_copy(src_ref=ref, dst_ref=ref, send_sem=z_send.at[number, part], recv_sem=z_recv.at[number, part], device_id={"tp": peer}, device_id_type=MESH))
+            if part == 0:
+                ref = b_all.at[2 * source + core]
+                copies.append(pltpu.make_async_remote_copy(src_ref=ref, dst_ref=ref, send_sem=zb_send.at[number], recv_sem=zb_recv.at[number], device_id={"tp": peer}, device_id_type=MESH))
+        return copies
+
+    def z_onward(number):
+        if number == 0:
+            return [(later, (0, 1)) for later in (1, 2) if later < chips - 1] or [(chips - 1, (0, 1))]
+        if number + 2 < chips - 1:
+            return [(number + 2, (0, 1))]
+        if number < chips - 1:
+            return [(chips - 1, (number % 2 == 0,))]
+        return []
+
+    def z_start(later, parts):
+        copies = z_copies(later)
+        for part in parts:
+            if part == 0:
+                copies[0].start()
+                copies[1].start()
+            else:
+                copies[2].start()
+
+    def axes(part):
+        return (0, 1) if part == 0 else (1, 0)
+
+    def sign_of(number):
+        return 1 - 2 * (number % 2)
+
+    def line_copy(number, part, hop):
+        axis, sign = axes(part)[0], sign_of(number)
+        source = group_at(axis, lax.rem(at[axis] + plane[axis] - sign * hop, plane[axis]), at[1 - axis])
+        ref = block(number, (part * dp + source) * unit, unit, core)
+        return pltpu.make_async_remote_copy(src_ref=ref, dst_ref=ref, send_sem=line_send.at[number, part, hop], recv_sem=line_recv.at[number, part, hop], device_id={"dp": beside(axis, sign)}, device_id_type=MESH)
+
+    def plane_copy(number, part, off, hop):
+        (one, two), sign = axes(part), sign_of(number)
+        source = group_at(one, lax.rem(at[one] + plane[one] - sign * off, plane[one]), lax.rem(at[two] + plane[two] - sign * hop, plane[two]))
+        ref = block(number, (part * dp + source) * unit, unit, core)
+        return pltpu.make_async_remote_copy(src_ref=ref, dst_ref=ref, send_sem=plane_send.at[number, part, off, hop], recv_sem=plane_recv.at[number, part, off, hop], device_id={"dp": beside(two, sign)}, device_id_type=MESH)
+
+    def w_pair(number, who):
+        ref = block(number, 0, rows, who)
+        bias = b_all.at[2 * shard_of_round(chip, chips, number) + who]
+        return [
+            pltpu.make_async_remote_copy(src_ref=ref, dst_ref=ref, send_sem=w_send.at[number], recv_sem=w_recv.at[number], device_id={"tp": partner}, device_id_type=MESH),
+            pltpu.make_async_remote_copy(src_ref=bias, dst_ref=bias, send_sem=wb_send.at[number], recv_sem=wb_recv.at[number], device_id={"tp": partner}, device_id_type=MESH),
+        ]
+
+    def gather(kind, number, hop):
+        if kind == "pass":
+            if number > 0:
+                for copy in z_copies(number):
+                    copy.wait_recv()
+            for later, parts in z_onward(number):
+                z_start(later, parts)
+            for part in range(2):
+                if number > 0 and plane[axes(part)[0]] > 1:
+                    line_copy(number, part, 0).start()
+            for part in range(2):
+                if number > 0 and plane[axes(part)[1]] > 1:
+                    plane_copy(number, part, 0, 0).start()
+        for part in range(2):
+            one, two = (plane[axis] for axis in axes(part))
+            if kind == "line" and hop < one:
+                line_copy(number, part, hop - 1).wait_recv()
+                if hop < one - 1:
+                    line_copy(number, part, hop).start()
+                if two > 1:
+                    plane_copy(number, part, hop, 0).start()
+            if kind == "plane" and hop < two:
+                for off in range(one):
+                    plane_copy(number, part, off, hop - 1).wait_recv()
+                    if hop < two - 1:
+                        plane_copy(number, part, off, hop).start()
+        if kind == "pair":
+            for copy in w_pair(number, core):
+                copy.start()
 
     def x_copies(item):
         way = lax.rem(item, 2)
@@ -103,8 +250,21 @@
             device_id={"tp": left if way else right}, device_id_type=MESH,
         )
 
+    for layer in (1, 0):
+        for copy in loads(layer):
+            copy.start()
     for copy in x_copies(0):
         copy.start()
+    b_all[me] = jnp.broadcast_to(b_ref[1:2].astype(jnp.float32), b_all.shape[1:])
+    turn_up(1)
+    own_copy = pltpu.make_async_copy(pack.at[1], w_all.at[pl.ds(pl.multiple_of(me * rows, 8), rows)], own_sem)
+    own_copy.start()
+    turn_up(0)
+    own_copy.wait()
+    events = schedule_of(chips, plane)
+    ln_row = ln_ref[0:1].astype(jnp.float32)
+    b_row = b_ref[0:1].astype(jnp.float32)
+    bias_row = bo_ref[0:1].astype(jnp.float32) + bd_ref[0:1].astype(jnp.float32)
 
     def turn(index, carry):
         t = index - 2
@@ -143,7 +303,14 @@
                 def _():
                     own = x_buf[way, pl.ds(pl.multiple_of(half + sub * sub_rows, sub_rows), sub_rows)].astype(jnp.float32)
                     total = ring[chips - 1, way, sub].astype(jnp.float32) + local
-                    y_ref[pl.ds(pl.multiple_of(way * half + sub * sub_rows, sub_rows), sub_rows)] = (own + bias_ref[...] + total).astype(y_ref.dtype)
+                    y_ref[pl.ds(pl.multiple_of(way * half + sub * sub_rows, sub_rows), sub_rows)] = (own + bias_row + total).astype(y_ref.dtype)
+
+        for due, group_events in sorted(events.items()):
+            if due < items + 2:
+                @pl.when(index == due)
+                def _():
+                    for event in group_events:
+                        gather(*event)
 
         @pl.when(index < items)
         def _():
@@ -154,8 +321,8 @@
 
             for copy in x_copies(index):
                 copy.wait()
-            normed = norm_rows(x_buf[lax.rem(index, 2)].astype(jnp.float32), ln_ref[...])
-            part = branches(normed, w_ref, b_ref[...], q_ref[...], k_ref[...], seq_len, head_dim).astype(jnp.bfloat16)
+            normed = norm_rows(x_buf[lax.rem(index, 2)].astype(jnp.float32), ln_row)
+            part = branches(normed, pack.at[0], b_row, q_ref[0], k_ref[0], seq_len, head_dim).astype(jnp.bfloat16)
             to_partner[index] = part[:half]
             mine[lax.rem(index, 4)] = part[half:]
             pair_copy(index).start()
@@ -163,6 +330,25 @@
         return carry
 
     lax.fori_loop(0, items + 2, turn, 0)
+    for due, group_events in sorted(events.items()):
+        if due >= items + 2:
+            for event in group_events:
+                gather(*event)
+    for number in range(chips):
+        for copy in w_pair(number, core):
+            copy.wait_send()
+        for copy in w_pair(number, 1 - core):
+            copy.wait_recv()
+        for part in range(2 if number > 0 else 0):
+            one, two = (plane[axis] for axis in axes(part))
+            for hop in range(one - 1):
+                line_copy(number, part, hop).wait_send()
+            for hop in range(two - 1):
+                for off in range(one):
+                    plane_copy(number, part, off, hop).wait_send()
+        if number > 0:
+            for copy in z_copies(number):
+                copy.wait_send()
 
     def drain(item, carry):
         pair_copy(item).wait_send()
@@ -179,26 +365,18 @@
     lax.fori_loop(0, chips - 1, drain_ring, 0)
 
 
-def second_kernel(seq_len, head_dim, tp, dp, y_ref, w_hbm, ln_ref, bias_ref, q_ref, k_ref, out_ref, w_buf, h_ref, acc_ref, w_sem, ring_send, ring_recv, pair_send, pair_recv):
+def second_kernel(seq_len, head_dim, tp, y_ref, w_hbm, b_all, ln_ref, bo_ref, bd_ref, q_ref, k_ref, out_ref, w_buf, h_ref, acc_ref, w_sem, ring_send, ring_recv, pair_send, pair_recv):
     core, chip, right, left, partner = neighbours(tp)
     chips = tp // 2
     share = y_ref.shape[0]
     images = share // seq_len
-    rows = w_buf.shape[1] - 8
-    piece = rows // dp
+    rows = w_buf.shape[1]
     sub_rows = seq_len // 4
-    mlp = rows - 4 * head_dim - (rows - 4 * head_dim) // 2
-    enter((right, left, partner))
-
-    def w_copies(turn):
-        shard = lax.rem(turn, tp)
+    enter((("tp", right), ("tp", left), ("tp", partner)))
+
+    def w_copy(turn):
         slot = lax.rem(turn, 2)
-        copies = []
-        for part in range(dp):
-            base = (shard * dp + part) * (piece + 8)
-            copies.append((pl.multiple_of(base, 8), piece, part * piece, part))
-        copies.append((pl.multiple_of(shard * dp * (piece + 8) + piece, 8), 8, rows, dp))
-        return [pltpu.make_async_copy(w_hbm.at[pl.ds(src, n)], w_buf.at[slot, pl.ds(dst, n)], w_sem.at[slot, place]) for src, n, dst, place in copies]
+        return pltpu.make_async_copy(w_hbm.at[pl.ds(pl.multiple_of(lax.rem(turn, tp) * rows, 8), rows)], w_buf.at[slot], w_sem.at[slot])
 
     def chunk(image, way, sub, owner):
         offset = owner * share + image * seq_len + way * (2 * sub_rows) + sub * sub_rows
@@ -241,11 +419,10 @@
 
             pair_copy(image, way, sub, step + 1, core).start()
 
-    for copy in w_copies(0):
-        copy.start()
+    w_copy(0).start()
     start = y_ref[...].astype(jnp.float32)
-    h_ref[...] = norm_rows(start, ln_ref[...])
-    acc_ref[...] = start + bias_ref[...]
+    h_ref[...] = norm_rows(start, ln_ref[1:2].astype(jnp.float32))
+    acc_ref[...] = start + (bo_ref[1:2].astype(jnp.float32) + bd_ref[1:2].astype(jnp.float32))
 
     def turn(index, carry):
         image = index // tp
@@ -253,19 +430,16 @@
 
         @pl.when(index + 1 < images * tp)
         def _():
-            for copy in w_copies(index + 1):
-                copy.start()
+            w_copy(index + 1).start()
 
         @pl.when(jnp.logical_and(image > 0, lax.rem(shard, 2) == 0))
         def _():
             event(image - 1, shard // 2)
 
-        for copy in w_copies(index):
-            copy.wait()
+        w_copy(index).wait()
         slot = lax.rem(index, 2)
         span = pl.ds(pl.multiple_of(image * seq_len, seq_len), seq_len)
-        b_up = w_buf[slot, pl.ds(rows, 8)].astype(jnp.float32)[0:1, 0:mlp]
-        acc_ref[span] += branches(h_ref[span], w_buf.at[slot, pl.ds(0, rows)], b_up, q_ref[...], k_ref[...], seq_len, head_dim)
+        acc_ref[span] += branches(h_ref[span], w_buf.at[slot], b_all[shard][0:1], q_ref[1], k_ref[1], seq_len, head_dim)
 
         @pl.when(shard == tp - 1)
         def _():
@@ -328,55 +502,55 @@
         tokens = tokens_in.reshape(n_tokens, model_dim)
         f32, bf16 = jnp.float32, jnp.bfloat16
 
-        def packed(layer):
-            return jnp.concatenate([w_query[layer].T, w_key[layer].T, w_value[layer].T, w_up[layer].T, w_down[layer], w_out[layer]], axis=0)
-
-        pack0, pack1 = packed(0), packed(1)
-        rows = pack1.shape[0]
-        piece = rows // dp
-        bias_rows = jnp.pad(b_up[1:2], ((0, 7), (0, model_dim - mlp)))
-        mine = jnp.concatenate([lax.dynamic_slice_in_dim(pack1, lax.axis_index("dp") * piece, piece, 0), bias_rows], axis=0)
-        pack0, mine = lax.optimization_barrier((pack0, mine))
-        gathered = lax.all_gather(mine, ("tp", "dp"), axis=0, tiled=True)
-        bias = (b_out.astype(f32) + b_down.astype(f32)).reshape(-1, 1, model_dim)
-        ln_rows = ln_scale.astype(f32).reshape(-1, 1, model_dim)
+        rows = 4 * head_dim + 2 * mlp
+        plane = plane_of(dp)
+        side = max(plane)
         q_cols = q_scale.astype(f32).reshape(-1, head_dim, 1)
         k_cols = k_scale.astype(f32).reshape(-1, head_dim, 1)
+        turned = [jnp.swapaxes(weight, 1, 2) for weight in (w_query, w_key, w_value)]
         vmem = pl.BlockSpec(memory_space=pltpu.VMEM)
         hbm = pl.BlockSpec(memory_space=pl.ANY)
         dma = pltpu.SemaphoreType.DMA
         flops = 2 * n_tokens * model_dim * (rows + seq_len // 2)
-        middle = pl.pallas_call(
-            functools.partial(first_kernel, seq_len, head_dim, tp),
-            out_shape=jax.ShapeDtypeStruct((share, model_dim), bf16),
-            in_specs=[hbm] + [vmem] * 6,
-            out_specs=vmem,
+        middle, w_all, b_all = pl.pallas_call(
+            functools.partial(first_kernel, seq_len, head_dim, tp, dp),
+            out_shape=(
+                jax.ShapeDtypeStruct((share, model_dim), bf16),
+                jax.ShapeDtypeStruct((tp * rows, model_dim), bf16),
+                jax.ShapeDtypeStruct((tp, 8, mlp), f32),
+            ),
+            in_specs=[hbm] * 7 + [vmem] * 6,
+            out_specs=(vmem, hbm, vmem),
             scratch_shapes=[
+                pltpu.VMEM((2, rows, model_dim), bf16), pltpu.VMEM((2, model_dim, mlp), bf16),
                 pltpu.VMEM((2, share, model_dim), bf16),
                 pltpu.VMEM((chips, 2, 2, half // 2, model_dim), bf16),
                 pltpu.VMEM((tp, half, model_dim), bf16),
                 pltpu.VMEM((tp, half, model_dim), bf16),
                 pltpu.VMEM((4, half, model_dim), bf16),
-                dma((2, 2)), dma((chips - 1, 2, 2)), dma((chips - 1, 2, 2)), dma((tp,)), dma((tp,)),
+                dma((2, 6)), dma, dma((2, 2)), dma((chips - 1, 2, 2)), dma((chips - 1, 2, 2)), dma((tp,)), dma((tp,)),
+                dma((chips, 2)), dma((chips, 2)), dma((chips,)), dma((chips,)),
+                dma((chips, 2, side)), dma((chips, 2, side)), dma((chips, 2, side, side)), dma((chips, 2, side, side)),
+                dma((chips,)), dma((chips,)), dma((chips,)), dma((chips,)),
             ],
-            compiler_params=pltpu.CompilerParams(vmem_limit_bytes=VMEM_BYTES, collective_id=0, has_side_effects=True),
-            cost_estimate=pl.CostEstimate(flops=4 * flops, bytes_accessed=4 * n_tokens * model_dim, transcendentals=0),
+            compiler_params=pltpu.CompilerParams(vmem_limit_bytes=FIRST_VMEM, collective_id=0, has_side_effects=True),
+            cost_estimate=pl.CostEstimate(flops=flops, bytes_accessed=4 * n_tokens * model_dim, transcendentals=0),
             name="first_layer",
-        )(tokens, pack0, ln_rows[0], b_up[0:1].astype(f32), q_cols[0], k_cols[0], bias[0])
+        )(tokens, *turned, w_up, w_down, w_out, ln_scale, b_up, q_cols, k_cols, b_out, b_down)
         out = pl.pallas_call(
-            functools.partial(second_kernel, seq_len, head_dim, tp, dp),
+            functools.partial(second_kernel, seq_len, head_dim, tp),
             out_shape=jax.ShapeDtypeStruct((n_tokens, model_dim), bf16),
-            in_specs=[vmem, hbm] + [vmem] * 4,
+            in_specs=[vmem, hbm] + [vmem] * 6,
             out_specs=vmem,
             scratch_shapes=[
-                pltpu.VMEM((2, rows + 8, model_dim), bf16),
+                pltpu.VMEM((2, rows, model_dim), bf16),
                 pltpu.VMEM((share, model_dim), bf16), pltpu.VMEM((share, model_dim), f32),
-                dma((2, dp + 1)), dma((images, 2, 2, chips)), dma((images, 2, 2, chips)), dma((images, 2, 2, chips)), dma((images, 2, 2, chips)),
+                dma((2,)), dma((images, 2, 2, chips)), dma((images, 2, 2, chips)), dma((images, 2, 2, chips)), dma((images, 2, 2, chips)),
             ],
-            compiler_params=pltpu.CompilerParams(vmem_limit_bytes=VMEM_BYTES, collective_id=1, has_side_effects=True),
-            cost_estimate=pl.CostEstimate(flops=4 * flops, bytes_accessed=2 * tp * rows * model_dim, transcendentals=0),
+            compiler_params=pltpu.CompilerParams(vmem_limit_bytes=SECOND_VMEM, collective_id=1, has_side_effects=True),
+            cost_estimate=pl.CostEstimate(flops=flops, bytes_accessed=2 * tp * rows * model_dim, transcendentals=0),
             name="second_layer",
-        )(middle, gathered, ln_rows[1], bias[1], q_cols[1], k_cols[1])
+        )(middle, w_all, b_all, ln_scale, b_out, b_down, q_cols, k_cols)
         return out.reshape(n_images, seq_len, model_dim)
 
     return jax.shard_map(per_device, mesh=mesh, in_specs=in_specs, out_specs=P("dp", None, None), check_vma=False)

time: 359 us -> 261 us (0.73)
  waiting for transfers between devices: 72.4 us -> 0 us
  between operations: 13.6 us -> 0.05 us
  local copies, waits for them, and re-layouts: 22 us -> 15.4 us
  Pallas kernels: 249 us -> 243 us
    all_gather x1 -> x0, waiting for transfers between devices: 72.4 us -> none  [per_device(): gathered = lax.all_gather(mine, ('tp', 'dp'), axis=0, tiled=True)]
    pallas_call x2, Pallas kernels: 249 us -> 243 us  [the longest x1 132 us: per_device(): pl.pallas_call(functools.partial(first_kernel, seq_len, head_dim, tp, dp)...]
    unnamed x28 -> x21, local copies, waits for them, and re-layouts: 18.7 us -> 15.1 us
  transfers between devices with their start and end apart: 1 -> 0, of which waited for: 1 -> 0; matrix products, arithmetic and copies ran while one was open for 0% -> 0% of each run, Pallas kernels for 37% -> 0%
where the time goes in v3:
time: 261 us; the launch traced here: 260 us
  Pallas kernels  243 us (93%)
  local copies, waits for them, and re-layouts  15.4 us (6%)
    pallas_call x1, Pallas kernels, per_device(): pl.pallas_call(functools.partial(first_kernel, seq_len, head_dim, tp, dp)...  132 us
    pallas_call x1, Pallas kernels, per_device(): pl.pallas_call(functools.partial(second_kernel, seq_len, head_dim, tp), o...  111 us
    unnamed x21, local copies, waits for them, and re-layouts  15.1 us

profile of v3, /device:TPU:21, one launch (start us, length us, event | category | flops | bytes accessed | tf_op | source)
XLA Modules:
  0.0 259.8 jit_solution(13736555568014359100)
XLA Ops:
  0.0 0.7 bitcast_convert_fusion.1
  0.7 0.7 bitcast_convert_fusion
  1.3 0.1 copy.15.k_ref
  1.4 0.1 copy.14.q_ref
  1.5 0.0 copy-start
  1.5 1.2 copy-done
  2.8 0.0 copy-start.1
  2.8 1.2 copy-done.1
  4.0 0.0 copy-start.2
  4.0 0.9 copy-done.2
  4.9 0.0 copy-start.3
  4.9 0.9 copy-done.3
  5.9 0.0 copy-start.4
  5.9 0.9 copy-done.4
  6.8 0.0 copy-start.5
  6.8 0.9 copy-done.5
  7.8 0.0 copy-start.6
  7.8 0.7 copy-done.6
  8.5 0.0 copy-start.7
  8.5 0.7 copy-done.7
  9.2 0.0 copy-start.8
  9.2 0.7 copy-done.8
  9.9 0.0 copy-start.9
  9.9 0.7 copy-done.9
  10.5 132.5 %first_layer.1 = (bf16[512,1024]{1,0:T(8,128)(2,1)S(1)}, bf16[12288,1024]{1,0:T(8,128)(2,1)}, f32[16,8,256]{2,1,0:T(8,128)S(1)}) custom-call(bf16[8192,1024]{1,0:T(8,128)(2,1)} %bitcast.15, bf16[2,64,1024]{2,1,0:T(8,128)(2,1)S(1)} %bitcast.12, bf16[2,64,1024]{2,1,0:T(8,128)(2,1)S(1)} %bitcast.13, bf16[2,64,1024]{2,1,0:T(8,128)(2,1)S(1)} %bitcast.14, ...), custom_call_target="tpu_custom_call" | custom-call | flops 15032385536 | bytes 33554432 | tf_op jit(solution)/shard_map/first_layer/pallas_call | solution.py:515
  143.0 110.6 %second_layer.1 = bf16[8192,1024]{1,0:T(8,128)(2,1)S(1)} custom-call(bf16[512,1024]{1,0:T(8,128)(2,1)S(1)} %get-tuple-element.8.y_ref, bf16[12288,1024]{1,0:T(8,128)(2,1)} %get-tuple-element.9.w_hbm, f32[16,8,256]{2,1,0:T(8,128)S(1)} %get-tuple-element.10.b_all, bf16[2,1024]{1,0:T(2,128)(2,1)S(1)} %copy-done.6, bf16[2,1024]{1,0:T(2,128)(2,1)S(1)} %copy-done.7, ...), custom_call_target="tpu_custom_call" | custom-call | flops 15032385536 | bytes 25165824 | tf_op jit(solution)/shard_map/second_layer/pallas_call | solution.py:540
  253.6 6.2 %copy.19 = bf16[32,256,1024]{2,1,0:T(8,128)(2,1)} copy(bf16[32,256,1024]{2,1,0:T(8,128)(2,1)S(1)} %bitcast.11) | data formatting | bytes 33554432
Async XLA Ops:
  1.5 1.2 copy-start
  2.8 1.2 copy-start.1
  4.0 0.9 copy-start.2
  4.9 0.9 copy-start.3
  5.9 0.9 copy-start.4
  6.8 0.9 copy-start.5
  7.8 0.7 copy-start.6
  8.5 0.7 copy-start.7
  9.2 0.7 copy-start.8
  9.9 0.7 copy-start.9

commit v4 on v3

v4 whole, which is shorter than its diff:
```python
import functools
import math

import jax
import jax.numpy as jnp
from jax import lax
from jax.experimental import pallas as pl
from jax.experimental.pallas import tpu as pltpu
from jax.sharding import PartitionSpec as P

LN_EPS = 1e-6
LOG2E = 1.4426950408889634
VMEM_BYTES = 45 * 1024 * 1024
LEAD = 3
MESH = pl.DeviceIdType.MESH


def norm_rows(values, scale_row):
    mean_val = jnp.mean(values, axis=-1, keepdims=True)
    centered = values - mean_val
    variance = jnp.mean(centered * centered, axis=-1, keepdims=True)
    return (centered * lax.rsqrt(variance + LN_EPS) * scale_row).astype(jnp.bfloat16)


def norm_cols(values, scale_col):
    mean_val = jnp.mean(values, axis=0, keepdims=True)
    centered = values - mean_val
    variance = jnp.mean(centered * centered, axis=0, keepdims=True)
    return (centered * lax.rsqrt(variance + LN_EPS) * scale_col).astype(jnp.bfloat16)


def branches(normed, w_ref, b_up, q_col, k_col, seq_len, head_dim):
    tokens = normed.shape[0]
    mlp = b_up.shape[1]
    qkv = 3 * head_dim
    up_end = qkv + mlp
    proj = lax.dot_general(w_ref[0:qkv], normed, (((1,), (1,)), ((), ())), preferred_element_type=jnp.float32)
    queries = norm_cols(proj[0:head_dim], q_col)
    keys_all = norm_cols(proj[head_dim : 2 * head_dim], k_col)
    values_all = proj[2 * head_dim : qkv].astype(jnp.bfloat16)
    pre_act = lax.dot_general(normed, w_ref[qkv:up_end], (((1,), (1,)), ((), ())), preferred_element_type=jnp.float32)
    activated = jax.nn.gelu(pre_act + b_up, approximate=True).astype(jnp.bfloat16)
    mixed = []
    for img in range(tokens // seq_len):
        cols = slice(img * seq_len, (img + 1) * seq_len)
        scores = lax.dot_general(keys_all[:, cols], queries[:, cols], (((0,), (0,)), ((), ())), preferred_element_type=jnp.float32)
        top = jnp.max(scores, axis=0, keepdims=True)
        expd = jnp.exp2((scores - top) * (LOG2E * head_dim**-0.5))
        prob = (expd * (1.0 / jnp.sum(expd, axis=0, keepdims=True))).astype(jnp.bfloat16)
        mixed.append(jnp.dot(values_all[:, cols], prob, preferred_element_type=jnp.float32))
    mixed_rows = jnp.concatenate(mixed, axis=1).T.astype(jnp.bfloat16)
    both = jnp.concatenate([activated, mixed_rows], axis=1)
    return jnp.dot(both, w_ref[up_end:], preferred_element_type=jnp.float32)


def neighbours(tp):
    me = lax.axis_index("tp")
    chips = tp // 2
    core = lax.rem(me, 2)
    chip = me // 2
    right = lax.rem(chip + 1, chips) * 2 + core
    left = lax.rem(chip + chips - 1, chips) * 2 + core
    return core, chip, right, left, me + 1 - 2 * core


def enter(peers):
    barrier = pltpu.get_barrier_semaphore()
    for axis, peer in peers:
        pl.semaphore_signal(barrier, inc=1, device_id={axis: peer}, device_id_type=MESH)
    pl.semaphore_wait(barrier, len(peers))


def plane_of(dp):
    side = math.isqrt(dp)
    return (side, side) if side * side == dp else (1, dp)


def shard_of_round(chip, chips, number):
    sign = 1 - 2 * (number % 2)
    return lax.rem(chip + chips + sign * ((number + 1) // 2), chips)


def schedule_of(chips, plane):
    side = max(plane)
    events = {0: [("pass", 0, 0), ("pair", 0, 0)]}
    for number in range(1, chips):
        begin = 4 + (7 * (number - 1)) // 2 if side < 3 else 3 * number
        events.setdefault(begin, []).append(("pass", number, 0))
        for hop in range(1, side):
            events.setdefault(begin + 2 + hop, []).append(("line", number, hop))
        for hop in range(1, side):
            events.setdefault(begin + 2 + side + hop, []).append(("plane", number, hop))
        events.setdefault(begin + 1 + 2 * side, []).append(("pair", number, 0))
    return events


def layers_kernel(
    seq_len, head_dim, tp, dp,
    x_hbm, wq_hbm, wk_hbm, wv_hbm, wup_hbm, wdown_hbm, wout_hbm, ln_hbm, bo_hbm, bd_hbm, bup_hbm, q_hbm, k_hbm,
    out_ref, w_all,
    ln_ref, bo_ref, bd_ref, bup_ref, q_ref, k_ref, pack, up_raw, x_buf, own_x, ring, from_partner, to_partner, mine, b_all, w_buf, h_ref, acc_ref,
    load_sem, small_sem, own_sem, x_sem, ring_send, ring_recv, pair_send, pair_recv, z_send, z_recv, zb_send, zb_recv,
    line_send, line_recv, plane_send, plane_recv, w_send, w_recv, wb_send, wb_recv, wl_sem, out_send, out_recv, outp_send, outp_recv,
):
    core, chip, right, left, partner = neighbours(tp)
    chips = tp // 2
    me = 2 * chip + core
    rows = pack.shape[1]
    mlp = up_raw.shape[2]
    qkv = 3 * head_dim
    share = own_x.shape[0]
    images = share // seq_len
    quarter = seq_len // 4
    half = seq_len // 2
    f32 = jnp.float32
    plane = plane_of(dp)
    group = lax.axis_index("dp")
    at = (group // plane[1], lax.rem(group, plane[1]))
    unit = rows // (2 * dp)

    def group_at(axis, pos, other):
        return pos * plane[1] + other if axis == 0 else other * plane[1] + pos

    def beside(axis, sign):
        return group_at(axis, lax.rem(at[axis] + plane[axis] + sign, plane[axis]), at[1 - axis])

    def loads(layer):
        pieces = [(wq_hbm, pack.at[layer, 0:head_dim]), (wk_hbm, pack.at[layer, head_dim : 2 * head_dim]), (wv_hbm, pack.at[layer, 2 * head_dim : qkv]), (wup_hbm, up_raw.at[layer]), (wdown_hbm, pack.at[layer, qkv + mlp : qkv + 2 * mlp]), (wout_hbm, pack.at[layer, qkv + 2 * mlp : rows])]
        return [pltpu.make_async_copy(src.at[layer], dst, load_sem.at[layer, place]) for place, (src, dst) in enumerate(pieces)]

    def turn_up(layer):
        for copy in loads(layer):
            copy.wait()
        pack[layer, qkv : qkv + mlp] = up_raw[layer].T

    small = [(ln_hbm, ln_ref), (bo_hbm, bo_ref), (bd_hbm, bd_ref), (bup_hbm, bup_ref), (q_hbm, q_ref), (k_hbm, k_ref)]
    small = [pltpu.make_async_copy(src, dst, small_sem.at[place]) for place, (src, dst) in enumerate(small)]

    def column(ref, layer):
        row = ref[layer : layer + 1].astype(f32)
        return jnp.broadcast_to(row, (8, head_dim)).T[:, 0:1]

    def block(number, start, count, owner):
        base = (2 * shard_of_round(chip, chips, number) + owner) * rows + start
        return w_all.at[pl.ds(pl.multiple_of(base, 8), count)]

    def z_copies(number):
        copies = []
        for part in range(2):
            rightwards = (part == 0) if number == chips - 1 else number % 2 == 1
            hops = (number + 1) // 2
            source = lax.rem(chip + chips + (1 - hops if rightwards else hops - 1), chips)
            peer = right if rightwards else left
            ref = w_all.at[pl.ds(pl.multiple_of((2 * source + core) * rows + (part * dp + group) * unit, 8), unit)]
            copies.append(pltpu.make_async_remote_copy(src_ref=ref, dst_ref=ref, send_sem=z_send.at[number, part], recv_sem=z_recv.at[number, part], device_id={"tp": peer}, device_id_type=MESH))
            if part == 0:
                ref = b_all.at[2 * source + core]
                copies.append(pltpu.make_async_remote_copy(src_ref=ref, dst_ref=ref, send_sem=zb_send.at[number], recv_sem=zb_recv.at[number], device_id={"tp": peer}, device_id_type=MESH))
        return copies

    def z_onward(number):
        if number == 0:
            return [(later, (0, 1)) for later in (1, 2) if later < chips - 1] or [(chips - 1, (0, 1))]
        if number + 2 < chips - 1:
            return [(number + 2, (0, 1))]
        if number < chips - 1:
            return [(chips - 1, (number % 2 == 0,))]
        return []

    def z_start(later, parts):
        copies = z_copies(later)
        for part in parts:
            if part == 0:
                copies[0].start()
                copies[1].start()
            else:
                copies[2].start()

    def axes(part):
        return (0, 1) if part == 0 else (1, 0)

    def sign_of(number):
        return 1 - 2 * (number % 2)

    def line_copy(number, part, hop):
        axis, sign = axes(part)[0], sign_of(number)
        source = group_at(axis, lax.rem(at[axis] + plane[axis] - sign * hop, plane[axis]), at[1 - axis])
        ref = block(number, (part * dp + source) * unit, unit, core)
        return pltpu.make_async_remote_copy(src_ref=ref, dst_ref=ref, send_sem=line_send.at[number, part, hop], recv_sem=line_recv.at[number, part, hop], device_id={"dp": beside(axis, sign)}, device_id_type=MESH)

    def plane_copy(number, part, off, hop):
        (one, two), sign = axes(part), sign_of(number)
        source = group_at(one, lax.rem(at[one] + plane[one] - sign * off, plane[one]), lax.rem(at[two] + plane[two] - sign * hop, plane[two]))
        ref = block(number, (part * dp + source) * unit, unit, core)
        return pltpu.make_async_remote_copy(src_ref=ref, dst_ref=ref, send_sem=plane_send.at[number, part, off, hop], recv_sem=plane_recv.at[number, part, off, hop], device_id={"dp": beside(two, sign)}, device_id_type=MESH)

    def w_pair(number, who):
        ref = block(number, 0, rows, who)
        bias = b_all.at[2 * shard_of_round(chip, chips, number) + who]
        return [
            pltpu.make_async_remote_copy(src_ref=ref, dst_ref=ref, send_sem=w_send.at[number], recv_sem=w_recv.at[number], device_id={"tp": partner}, device_id_type=MESH),
            pltpu.make_async_remote_copy(src_ref=bias, dst_ref=bias, send_sem=wb_send.at[number], recv_sem=wb_recv.at[number], device_id={"tp": partner}, device_id_type=MESH),
        ]

    def gather(kind, number, hop):
        if kind == "pass":
            if number > 0:
                for copy in z_copies(number):
                    copy.wait_recv()
            for later, parts in z_onward(number):
                z_start(later, parts)
            for part in range(2):
                if number > 0 and plane[axes(part)[0]] > 1:
                    line_copy(number, part, 0).start()
            for part in range(2):
                if number > 0 and plane[axes(part)[1]] > 1:
                    plane_copy(number, part, 0, 0).start()
        for part in range(2):
            one, two = (plane[axis] for axis in axes(part))
            if kind == "line" and hop < one:
                line_copy(number, part, hop - 1).wait_recv()
                if hop < one - 1:
                    line_copy(number, part, hop).start()
                if two > 1:
                    plane_copy(number, part, hop, 0).start()
            if kind == "plane" and hop < two:
                for off in range(one):
                    plane_copy(number, part, off, hop - 1).wait_recv()
                    if hop < two - 1:
                        plane_copy(number, part, off, hop).start()
        if kind == "pair":
            for copy in w_pair(number, core):
                copy.start()

    def place_of(item):
        image, number = item // chips, lax.rem(item, chips)
        near, odd, own = number // 2, lax.rem(number, 2), number // (chips - 1)
        far = chips - 2 - near
        there = lax.rem(chip + 2 * chips + (2 * odd - 1) * (1 + near) * (1 - own), chips)
        upper = (near * (1 - odd) + far * odd) * (1 - own) + (chips - 1) * own
        lower = (near * odd + far * (1 - odd)) * (1 - own) + (chips - 1) * own
        return image, there, (upper, lower)

    def x_copies(item):
        image, there, _ = place_of(item)
        slot = lax.rem(item, 2)
        return [
            pltpu.make_async_copy(
                x_hbm.at[pl.ds(pl.multiple_of((2 * there + owner) * share + image * seq_len, seq_len), seq_len)],
                x_buf.at[slot, pl.ds(place * seq_len, seq_len)],
                x_sem.at[slot, place],
            )
            for place, owner in ((0, 1 - core), (1, core))
        ]

    def pair_copies(item):
        image, _, steps = place_of(item)
        return [
            pltpu.make_async_remote_copy(
                src_ref=to_partner.at[lax.rem(item, 4), way], dst_ref=from_partner.at[image, way, steps[way]],
                send_sem=pair_send.at[image, way, steps[way]], recv_sem=pair_recv.at[image, way, steps[way]],
                device_id={"tp": partner}, device_id_type=MESH,
            )
            for way in range(2)
        ]

    def pair_arrival(image, way, step):
        return pltpu.make_async_remote_copy(
            src_ref=to_partner.at[0, way], dst_ref=from_partner.at[image, way, step],
            send_sem=pair_send.at[image, way, step], recv_sem=pair_recv.at[image, way, step],
            device_id={"tp": partner}, device_id_type=MESH,
        )

    def ring_copy(image, step, way, sub):
        return pltpu.make_async_remote_copy(
            src_ref=ring.at[image, step, way, sub], dst_ref=ring.at[image, step + 1, way, sub],
            send_sem=ring_send.at[image, step, way, sub], recv_sem=ring_recv.at[image, step, way, sub],
            device_id={"tp": left if way else right}, device_id_type=MESH,
        )

    def w_copy(turn):
        shard = lax.rem(turn, tp)
        slot = lax.rem(turn, 2)
        return pltpu.make_async_copy(block(shard // 2, 0, rows, whose(shard)), w_buf.at[slot], wl_sem.at[slot])

    def whose(shard):
        odd = lax.rem(shard, 2)
        return core + odd - 2 * core * odd

    def chunk(image, way, sub, owner):
        offset = owner * share + image * seq_len + way * (2 * quarter) + sub * quarter
        return out_ref.at[pl.ds(pl.multiple_of(offset, quarter), quarter)]

    def origin(way, step):
        back = chip - step if way == 0 else chip + step
        return 2 * lax.rem(back + chips, chips)

    def out_copy(image, way, sub, step):
        ref = chunk(image, way, sub, origin(way, step) + core)
        return pltpu.make_async_remote_copy(
            src_ref=ref, dst_ref=ref, send_sem=out_send.at[image, way, sub, step], recv_sem=out_recv.at[image, way, sub, step],
            device_id={"tp": left if way else right}, device_id_type=MESH,
        )

    def arrival(image, way, sub, step):
        ref = chunk(image, way, sub, origin(way, step + 1) + core)
        return pltpu.make_async_remote_copy(
            src_ref=ref, dst_ref=ref, send_sem=out_send.at[image, way, sub, step], recv_sem=out_recv.at[image, way, sub, step],
            device_id={"tp": left if way else right}, device_id_type=MESH,
        )

    def out_pair(image, way, sub, step, who):
        ref = chunk(image, way, sub, origin(way, step) + who)
        return pltpu.make_async_remote_copy(
            src_ref=ref, dst_ref=ref, send_sem=outp_send.at[image, way, sub, step], recv_sem=outp_recv.at[image, way, sub, step],
            device_id={"tp": partner}, device_id_type=MESH,
        )

    def event(image, number):
        step = number // 2
        sub = lax.rem(number, 2)
        for way in range(2):
            arrival(image, way, sub, step).wait_recv()

            @pl.when(step + 1 < chips - 1)
            def _():
                out_copy(image, way, sub, step + 1).start()

            out_pair(image, way, sub, step + 1, core).start()

    peers = [("tp", right), ("tp", left), ("tp", partner)]
    for axis in range(2):
        peers += [("dp", beside(axis, sign)) for sign in (1, -1)[: min(plane[axis] - 1, 2)]]
    enter(peers)

    for layer in (1, 0):
        for copy in loads(layer):
            copy.start()
        if layer == 1:
            for copy in small:
                copy.start()
    for copy in x_copies(0):
        copy.start()
    own_load = pltpu.make_async_copy(x_hbm.at[pl.ds(pl.multiple_of(me * share, share), share)], own_x, own_sem.at[1])
    own_load.start()
    for copy in small:
        copy.wait()
    b_all[me] = jnp.broadcast_to(bup_ref[1:2].astype(f32), b_all.shape[1:])
    turn_up(1)
    own_copy = pltpu.make_async_copy(pack.at[1], w_all.at[pl.ds(pl.multiple_of(me * rows, 8), rows)], own_sem.at[0])
    own_copy.start()
    turn_up(0)
    own_copy.wait()
    own_load.wait()
    events = schedule_of(chips, plane)
    ln_rows = [ln_ref[layer : layer + 1].astype(f32) for layer in range(2)]
    bias_rows = [bo_ref[layer : layer + 1].astype(f32) + bd_ref[layer : layer + 1].astype(f32) for layer in range(2)]
    b_row = bup_ref[0:1].astype(f32)
    q_cols = [column(q_ref, layer) for layer in range(2)]
    k_cols = [column(k_ref, layer) for layer in range(2)]
    items = images * chips
    ready = [due - 2 * number + 1 for due, due_events in events.items() for kind, number, _ in due_events if kind == "pair"]
    second = max([LEAD + items] + ready)

    def turn(index, carry):
        t = index - LEAD

        @pl.when(jnp.logical_and(t >= 0, t < 2 * items))
        def _():
            image = t // (2 * chips)
            step = lax.rem(t, 2 * chips) // 2
            sub = lax.rem(t, 2)
            span = pl.ds(pl.multiple_of(sub * quarter, quarter), quarter)
            for way in range(2):
                @pl.when(sub == 0)
                def _():
                    pair_arrival(image, way, step).wait_recv()

                local = from_partner[image, way, step, span].astype(f32) + mine[image, way, step, span].astype(f32)

                @pl.when(step == 0)
                def _():
                    ring[image, 0, way, sub] = local.astype(ring.dtype)

                @pl.when(step > 0)
                def _():
                    ring_copy(image, step - 1, way, sub).wait_recv()

                @pl.when(jnp.logical_and(step > 0, step < chips - 1))
                def _():
                    ring[image, step, way, sub] = (ring[image, step, way, sub].astype(f32) + local).astype(ring.dtype)

                @pl.when(step < chips - 1)
                def _():
                    ring_copy(image, step, way, sub).start()

                @pl.when(step == chips - 1)
                def _():
                    here = pl.ds(pl.multiple_of(image * seq_len + way * half + sub * quarter, quarter), quarter)
                    total = ring[image, chips - 1, way, sub].astype(f32) + local
                    middle = (own_x[here].astype(f32) + bias_rows[0] + total).astype(jnp.bfloat16).astype(f32)
                    h_ref[here] = norm_rows(middle, ln_rows[1])
                    acc_ref[here] = middle + bias_rows[1]

        for due, due_events in sorted(events.items()):
            @pl.when(index == due)
            def _():
                for event_args in due_events:
                    gather(*event_args)

        @pl.when(index < items)
        def _():
            @pl.when(index + 1 < items)
            def _():
                for copy in x_copies(index + 1):
                    copy.start()

            @pl.when(index >= 4)
            def _():
                for copy in pair_copies(index - 4):
                    copy.wait_send()

            for copy in x_copies(index):
                copy.wait()
            normed = norm_rows(x_buf[lax.rem(index, 2)].astype(f32), ln_rows[0])
            part = branches(normed, pack.at[0], b_row, q_cols[0], k_cols[0], seq_len, head_dim).astype(jnp.bfloat16)
            image, _, steps = place_of(index)
            for way in range(2):
                to_partner[lax.rem(index, 4), way] = part[way * half : (way + 1) * half]
                mine[image, way, steps[way]] = part[seq_len + way * half : seq_len + (way + 1) * half]
            for copy in pair_copies(index):
                copy.start()

        @pl.when(index == second - 1)
        def _():
            w_copy(0).start()

        @pl.when(index >= second)
        def _():
            m = index - second
            image = m // tp
            shard = lax.rem(m, tp)

            @pl.when(jnp.logical_and(image > 0, lax.rem(shard, 2) == 0))
            def _():
                event(image - 1, shard // 2)

            for number in range(chips):
                @pl.when(m == 2 * number)
                def _():
                    for copy in w_pair(number, 1 - core):
                        copy.wait_recv()

            @pl.when(m + 1 < images * tp)
            def _():
                w_copy(m + 1).start()

            w_copy(m).wait()
            slot = lax.rem(m, 2)
            span = pl.ds(pl.multiple_of(image * seq_len, seq_len), seq_len)
            owner = 2 * shard_of_round(chip, chips, shard // 2) + whose(shard)
            acc_ref[span] += branches(h_ref[span], w_buf.at[slot], b_all[owner][0:1], q_cols[1], k_cols[1], seq_len, head_dim)

            @pl.when(shard == tp - 1)
            def _():
                out_ref[pl.ds(pl.multiple_of(me * share + image * seq_len, seq_len), seq_len)] = acc_ref[span].astype(out_ref.dtype)
                for sub in range(2):
                    for way in range(2):
                        out_copy(image, way, sub, 0).start()
                for sub in range(2):
                    for way in range(2):
                        out_pair(image, way, sub, 0, core).start()

        return carry

    lax.fori_loop(0, second + images * tp, turn, 0)
    total = 2 * (chips - 1)
    done = tp // 2

    def tail(number, carry):
        @pl.when(number + done < total)
        def _():
            event(images - 2, number + done)

        event(images - 1, number)
        return carry

    lax.fori_loop(0, total, tail, 0)

    def drain(step, carry):
        for image in range(images):
            for way in range(2):
                for sub in range(2):
                    @pl.when(step < chips - 1)
                    def _():
                        ring_copy(image, step, way, sub).wait_send()
                        out_copy(image, way, sub, step).wait_send()

                    out_pair(image, way, sub, step, core).wait_send()
                    out_pair(image, way, sub, step, 1 - core).wait_recv()
        return carry

    lax.fori_loop(0, chips, drain, 0)
    for item in range(max(items - 4, 0), items):
        for copy in pair_copies(item):
            copy.wait_send()
    for number in range(chips):
        for copy in w_pair(number, core):
            copy.wait_send()
        for part in range(2 if number > 0 else 0):
            one, two = (plane[axis] for axis in axes(part))
            for hop in range(one - 1):
                line_copy(number, part, hop).wait_send()
            for hop in range(two - 1):
                for off in range(one):
                    plane_copy(number, part, off, hop).wait_send()
        if number > 0:
            for copy in z_copies(number):
                copy.wait_send()


def solution(mesh):
    col_spec = P(None, None, "tp")
    row_spec = P(None, "tp", None)
    in_specs = (P("dp", None, None), P(), col_spec, col_spec, col_spec, P(), P(), row_spec, P(), col_spec, P(None, "tp"), row_spec, P())
    tp = mesh.shape["tp"]
    dp = mesh.shape["dp"]
    chips = tp // 2

    def per_device(tokens_in, ln_scale, w_query, w_key, w_value, q_scale, k_scale, w_out, b_out, w_up, b_up, w_down, b_down):
        n_images, seq_len, model_dim = tokens_in.shape
        n_tokens = n_images * seq_len
        head_dim = q_scale.shape[1]
        mlp = w_up.shape[2]
        share = n_tokens // tp
        images = share // seq_len
        half, quarter = seq_len // 2, seq_len // 4
        rows = 4 * head_dim + 2 * mlp
        side = max(plane_of(dp))
        bf16, f32 = jnp.bfloat16, jnp.float32
        turned = [jnp.swapaxes(weight, 1, 2) for weight in (w_query, w_key, w_value)]
        hbm = pl.BlockSpec(memory_space=pltpu.HBM)
        vmem, dma = pltpu.VMEM, pltpu.SemaphoreType.DMA
        layers = ln_scale.shape[0]
        operands = (tokens_in.reshape(n_tokens, model_dim), *turned, w_up, w_down, w_out, ln_scale, b_out, b_down, b_up, q_scale, k_scale)
        out, _ = pl.pallas_call(
            functools.partial(layers_kernel, seq_len, head_dim, tp, dp),
            out_shape=(vmem((n_tokens, model_dim), bf16), jax.ShapeDtypeStruct((tp * rows, model_dim), bf16)),
            in_specs=[hbm] * 13,
            out_specs=(pl.BlockSpec(memory_space=pltpu.VMEM), hbm),
            scratch_shapes=[
                vmem((layers, model_dim), bf16), vmem((layers, model_dim), bf16), vmem((layers, model_dim), bf16), vmem((layers, mlp), bf16), vmem((layers, head_dim), bf16), vmem((layers, head_dim), bf16),
                vmem((layers, rows, model_dim), bf16), vmem((layers, model_dim, mlp), bf16),
                vmem((2, 2 * seq_len, model_dim), bf16), vmem((share, model_dim), bf16),
                vmem((images, chips, 2, 2, quarter, model_dim), bf16),
                vmem((images, 2, chips, half, model_dim), bf16), vmem((4, 2, half, model_dim), bf16), vmem((images, 2, chips, half, model_dim), bf16),
                vmem((tp, 8, mlp), f32), vmem((2, rows, model_dim), bf16), vmem((share, model_dim), bf16), vmem((share, model_dim), f32),
                dma((layers, 6)), dma((6,)), dma((2,)), dma((2, 2)),
                dma((images, chips, 2, 2)), dma((images, chips, 2, 2)), dma((images, 2, chips)), dma((images, 2, chips)),
                dma((chips, 2)), dma((chips, 2)), dma((chips,)), dma((chips,)),
                dma((chips, 2, side)), dma((chips, 2, side)), dma((chips, 2, side, side)), dma((chips, 2, side, side)),
                dma((chips,)), dma((chips,)), dma((chips,)), dma((chips,)), dma((2,)),
                dma((images, 2, 2, chips)), dma((images, 2, 2, chips)), dma((images, 2, 2, chips)), dma((images, 2, 2, chips)),
            ],
            compiler_params=pltpu.CompilerParams(vmem_limit_bytes=VMEM_BYTES, collective_id=0, has_side_effects=True),
            cost_estimate=pl.CostEstimate(flops=4 * n_tokens * model_dim * (rows + seq_len // 2), bytes_accessed=8 * n_tokens * model_dim, transcendentals=0),
            name="layers",
        )(*(pltpu.with_memory_space_constraint(value, pltpu.HBM) for value in operands))
        return out.reshape(n_images, seq_len, model_dim)

    return jax.shard_map(per_device, mesh=mesh, in_specs=in_specs, out_specs=P("dp", None, None), check_vma=False)
```

time: 261 us -> 239 us (0.916)
  Pallas kernels: 243 us -> 233 us
  local copies, waits for them, and re-layouts: 15.4 us -> 6.16 us
    pallas_call x2 -> x1, Pallas kernels: 243 us -> 233 us  [per_device(): pl.pallas_call(functools.partial(layers_kernel, seq_len, head_dim, tp, dp...]
    unnamed x21 -> x1, local copies, waits for them, and re-layouts: 15.1 us -> 6.16 us
where the time goes in v4:
time: 239 us
  Pallas kernels  233 us (97%)
  local copies, waits for them, and re-layouts  6.16 us (3%)
    pallas_call x1, Pallas kernels, per_device(): pl.pallas_call(functools.partial(layers_kernel, seq_len, head_dim, tp, dp...  233 us
    unnamed x1, local copies, waits for them, and re-layouts  6.16 us

profile of v4, /device:TPU:21, one launch (start us, length us, event | category | flops | bytes accessed | tf_op | source)
XLA Modules:
  0.0 238.8 jit_solution(2676031983408524898)
XLA Ops:
  0.0 232.6 %layers.1 = (bf16[8192,1024]{1,0:T(8,128)(2,1)S(1)}, bf16[12288,1024]{1,0:T(8,128)(2,1)}) custom-call(bf16[8192,1024]{1,0:T(8,128)(2,1)} %bitcast.6, bf16[2,64,1024]{2,1,0:T(8,128)(2,1)} %bitcast.7, bf16[2,64,1024]{2,1,0:T(8,128)(2,1)} %bitcast.8, bf16[2,64,1024]{2,1,0:T(8,128)(2,1)} %bitcast.9, bf16[2,1024,256]{2,1,0:T(8,128)(2,1)} %wup_hbm.1, ...), custom_call_target="tpu_custom_call" | custom-call | flops 30064771072 | bytes 67108864 | tf_op jit(solution)/shard_map/layers/pallas_call | solution.py:546
  232.6 6.2 %copy.15 = bf16[32,256,1024]{2,1,0:T(8,128)(2,1)} copy(bf16[32,256,1024]{2,1,0:T(8,128)(2,1)S(1)} %bitcast.5) | data formatting | bytes 33554432

commit v5 on v4

--- a/solution.py
+++ b/solution.py
@@ -82,12 +82,16 @@
 
 def schedule_of(chips, plane):
     side = max(plane)
-    events = {0: [("pass", 0, 0), ("pair", 0, 0)]}
+    events = {}
     for number in range(1, chips):
-        begin = 4 + (7 * (number - 1)) // 2 if side < 3 else 3 * number
+        begin = 4 + ((7 * (number - 1) + 1) // 2 if side < 3 else 3 * (number - 1))
+        if number % 2 == 1:
+            pair = (number + 1) // 2
+            events.setdefault(begin, []).extend([("came", pair, 0), ("onward", pair, 0)])
+            events.setdefault(begin + 2, []).append(("onward", pair, 1))
         events.setdefault(begin, []).append(("pass", number, 0))
         for hop in range(1, side):
-            events.setdefault(begin + 2 + hop, []).append(("line", number, hop))
+            events.setdefault(begin + 1 + hop, []).append(("line", number, hop))
         for hop in range(1, side):
             events.setdefault(begin + 2 + side + hop, []).append(("plane", number, hop))
         events.setdefault(begin + 1 + 2 * side, []).append(("pair", number, 0))
@@ -203,17 +207,22 @@
         ]
 
     def gather(kind, number, hop):
+        both = [each for each in (2 * number - 1, 2 * number) if each < chips]
+        if kind == "came":
+            for each in both:
+                for copy in z_copies(each):
+                    copy.wait_recv()
+        if kind == "onward":
+            for each in both:
+                for later, parts in z_onward(each):
+                    if hop in parts:
+                        z_start(later, (hop,))
         if kind == "pass":
-            if number > 0:
-                for copy in z_copies(number):
-                    copy.wait_recv()
-            for later, parts in z_onward(number):
-                z_start(later, parts)
             for part in range(2):
-                if number > 0 and plane[axes(part)[0]] > 1:
+                if plane[axes(part)[0]] > 1:
                     line_copy(number, part, 0).start()
             for part in range(2):
-                if number > 0 and plane[axes(part)[1]] > 1:
+                if plane[axes(part)[1]] > 1:
                     plane_copy(number, part, 0, 0).start()
         for part in range(2):
             one, two = (plane[axis] for axis in axes(part))
@@ -349,8 +358,11 @@
     turn_up(1)
     own_copy = pltpu.make_async_copy(pack.at[1], w_all.at[pl.ds(pl.multiple_of(me * rows, 8), rows)], own_sem.at[0])
     own_copy.start()
+    own_copy.wait()
+    for later, parts in z_onward(0):
+        z_start(later, parts)
+    gather("pair", 0, 0)
     turn_up(0)
-    own_copy.wait()
     own_load.wait()
     events = schedule_of(chips, plane)
     ln_rows = [ln_ref[layer : layer + 1].astype(f32) for layer in range(2)]

time: 239 us -> 231 us (0.967)
  Pallas kernels: 233 us -> 224 us
    pallas_call x1, Pallas kernels: 233 us -> 224 us  [per_device(): pl.pallas_call(functools.partial(layers_kernel, seq_len, head_dim, tp, dp...]
where the time goes in v5:
time: 231 us
  Pallas kernels  224 us (97%)
  local copies, waits for them, and re-layouts  6.16 us (3%)
    pallas_call x1, Pallas kernels, per_device(): pl.pallas_call(functools.partial(layers_kernel, seq_len, head_dim, tp, dp...  224 us
    unnamed x1, local copies, waits for them, and re-layouts  6.16 us

profile of v5, /device:TPU:21, one launch (start us, length us, event | category | flops | bytes accessed | tf_op | source)
XLA Modules:
  0.0 230.6 jit_solution(8075955634126675855)
XLA Ops:
  0.0 224.4 %layers.1 = (bf16[8192,1024]{1,0:T(8,128)(2,1)S(1)}, bf16[12288,1024]{1,0:T(8,128)(2,1)}) custom-call(bf16[8192,1024]{1,0:T(8,128)(2,1)} %bitcast.6, bf16[2,64,1024]{2,1,0:T(8,128)(2,1)} %bitcast.7, bf16[2,64,1024]{2,1,0:T(8,128)(2,1)} %bitcast.8, bf16[2,64,1024]{2,1,0:T(8,128)(2,1)} %bitcast.9, bf16[2,1024,256]{2,1,0:T(8,128)(2,1)} %wup_hbm.1, ...), custom_call_target="tpu_custom_call" | custom-call | flops 30064771072 | bytes 67108864 | tf_op jit(solution)/shard_map/layers/pallas_call | solution.py:558
  224.4 6.2 %copy.15 = bf16[32,256,1024]{2,1,0:T(8,128)(2,1)} copy(bf16[32,256,1024]{2,1,0:T(8,128)(2,1)S(1)} %bitcast.5) | data formatting | bytes 33554432

commit v6 on v5

--- a/solution.py
+++ b/solution.py
@@ -12,6 +12,9 @@
 LOG2E = 1.4426950408889634
 VMEM_BYTES = 45 * 1024 * 1024
 LEAD = 3
+COLUMNS = 256
+NORM_ROWS = 16
+WAIT = 2
 MESH = pl.DeviceIdType.MESH
 
 
@@ -29,7 +32,7 @@
     return (centered * lax.rsqrt(variance + LN_EPS) * scale_col).astype(jnp.bfloat16)
 
 
-def branches(normed, w_ref, b_up, q_col, k_col, seq_len, head_dim):
+def branches(normed, w_ref, b_up, q_col, k_col, seq_len, head_dim, emit, between=None):
     tokens = normed.shape[0]
     mlp = b_up.shape[1]
     qkv = 3 * head_dim
@@ -39,6 +42,8 @@
     keys_all = norm_cols(proj[head_dim : 2 * head_dim], k_col)
     values_all = proj[2 * head_dim : qkv].astype(jnp.bfloat16)
     pre_act = lax.dot_general(normed, w_ref[qkv:up_end], (((1,), (1,)), ((), ())), preferred_element_type=jnp.float32)
+    if between is not None:
+        between()
     activated = jax.nn.gelu(pre_act + b_up, approximate=True).astype(jnp.bfloat16)
     mixed = []
     for img in range(tokens // seq_len):
@@ -50,7 +55,9 @@
         mixed.append(jnp.dot(values_all[:, cols], prob, preferred_element_type=jnp.float32))
     mixed_rows = jnp.concatenate(mixed, axis=1).T.astype(jnp.bfloat16)
     both = jnp.concatenate([activated, mixed_rows], axis=1)
-    return jnp.dot(both, w_ref[up_end:], preferred_element_type=jnp.float32)
+    for start in range(0, w_ref.shape[1], COLUMNS):
+        cols = slice(start, min(start + COLUMNS, w_ref.shape[1]))
+        emit(cols, jnp.dot(both, w_ref[up_end:, cols], preferred_element_type=jnp.float32))
 
 
 def neighbours(tp):
@@ -102,7 +109,7 @@
     seq_len, head_dim, tp, dp,
     x_hbm, wq_hbm, wk_hbm, wv_hbm, wup_hbm, wdown_hbm, wout_hbm, ln_hbm, bo_hbm, bd_hbm, bup_hbm, q_hbm, k_hbm,
     out_ref, w_all,
-    ln_ref, bo_ref, bd_ref, bup_ref, q_ref, k_ref, pack, up_raw, x_buf, own_x, ring, from_partner, to_partner, mine, b_all, w_buf, h_ref, acc_ref,
+    ln_ref, bo_ref, bd_ref, bup_ref, q_ref, k_ref, pack, up_raw, x_buf, own_x, ring, from_partner, to_partner, mine, b_all, w_buf, h0_ref, h_ref, acc_ref,
     load_sem, small_sem, own_sem, x_sem, ring_send, ring_recv, pair_send, pair_recv, z_send, z_recv, zb_send, zb_recv,
     line_send, line_recv, plane_send, plane_recv, w_send, w_recv, wb_send, wb_recv, wl_sem, out_send, out_recv, outp_send, outp_recv,
 ):
@@ -348,8 +355,9 @@
         if layer == 1:
             for copy in small:
                 copy.start()
-    for copy in x_copies(0):
-        copy.start()
+    for item in range(2):
+        for copy in x_copies(item):
+            copy.start()
     own_load = pltpu.make_async_copy(x_hbm.at[pl.ds(pl.multiple_of(me * share, share), share)], own_x, own_sem.at[1])
     own_load.start()
     for copy in small:
@@ -370,6 +378,15 @@
     b_row = bup_ref[0:1].astype(f32)
     q_cols = [column(q_ref, layer) for layer in range(2)]
     k_cols = [column(k_ref, layer) for layer in range(2)]
+
+    def norm_item(item):
+        for start in range(0, 2 * seq_len, NORM_ROWS):
+            here = slice(start, start + NORM_ROWS)
+            h0_ref[here] = norm_rows(x_buf[lax.rem(item, 2), here].astype(f32), ln_rows[0])
+
+    for copy in x_copies(0):
+        copy.wait()
+    norm_item(0)
     items = images * chips
     ready = [due - 2 * number + 1 for due, due_events in events.items() for kind, number, _ in due_events if kind == "pair"]
     second = max([LEAD + items] + ready)
@@ -425,6 +442,11 @@
             @pl.when(index + 1 < items)
             def _():
                 for copy in x_copies(index + 1):
+                    copy.wait()
+
+            @pl.when(index + 2 < items)
+            def _():
+                for copy in x_copies(index + 2):
                     copy.start()
 
             @pl.when(index >= 4)
@@ -432,14 +454,15 @@
                 for copy in pair_copies(index - 4):
                     copy.wait_send()
 
-            for copy in x_copies(index):
-                copy.wait()
-            normed = norm_rows(x_buf[lax.rem(index, 2)].astype(f32), ln_rows[0])
-            part = branches(normed, pack.at[0], b_row, q_cols[0], k_cols[0], seq_len, head_dim).astype(jnp.bfloat16)
             image, _, steps = place_of(index)
-            for way in range(2):
-                to_partner[lax.rem(index, 4), way] = part[way * half : (way + 1) * half]
-                mine[image, way, steps[way]] = part[seq_len + way * half : seq_len + (way + 1) * half]
+
+            def emit(cols, part):
+                part = part.astype(jnp.bfloat16)
+                for way in range(2):
+                    to_partner[lax.rem(index, 4), way, :, cols] = part[way * half : (way + 1) * half]
+                    mine[image, way, steps[way], :, cols] = part[seq_len + way * half : seq_len + (way + 1) * half]
+
+            branches(h0_ref[...], pack.at[0], b_row, q_cols[0], k_cols[0], seq_len, head_dim, emit, lambda: norm_item(index + 1))
             for copy in pair_copies(index):
                 copy.start()
 
@@ -453,9 +476,11 @@
             image = m // tp
             shard = lax.rem(m, tp)
 
-            @pl.when(jnp.logical_and(image > 0, lax.rem(shard, 2) == 0))
-            def _():
-                event(image - 1, shard // 2)
+            late = shard - WAIT
+
+            @pl.when(jnp.logical_and(image > 0, jnp.logical_and(late >= 0, lax.rem(late, 4) < 3)))
+            def _():
+                event(image - 1, 3 * (late // 4) + lax.rem(late, 4))
 
             for number in range(chips):
                 @pl.when(m == 2 * number)
@@ -471,7 +496,11 @@
             slot = lax.rem(m, 2)
             span = pl.ds(pl.multiple_of(image * seq_len, seq_len), seq_len)
             owner = 2 * shard_of_round(chip, chips, shard // 2) + whose(shard)
-            acc_ref[span] += branches(h_ref[span], w_buf.at[slot], b_all[owner][0:1], q_cols[1], k_cols[1], seq_len, head_dim)
+
+            def emit(cols, part):
+                acc_ref[span, cols] += part
+
+            branches(h_ref[span], w_buf.at[slot], b_all[owner][0:1], q_cols[1], k_cols[1], seq_len, head_dim, emit)
 
             @pl.when(shard == tp - 1)
             def _():
@@ -487,7 +516,7 @@
 
     lax.fori_loop(0, second + images * tp, turn, 0)
     total = 2 * (chips - 1)
-    done = tp // 2
+    done = sum(late % 4 < 3 for late in range(tp - WAIT))
 
     def tail(number, carry):
         @pl.when(number + done < total)
@@ -566,7 +595,7 @@
                 vmem((2, 2 * seq_len, model_dim), bf16), vmem((share, model_dim), bf16),
                 vmem((images, chips, 2, 2, quarter, model_dim), bf16),
                 vmem((images, 2, chips, half, model_dim), bf16), vmem((4, 2, half, model_dim), bf16), vmem((images, 2, chips, half, model_dim), bf16),
-                vmem((tp, 8, mlp), f32), vmem((2, rows, model_dim), bf16), vmem((share, model_dim), bf16), vmem((share, model_dim), f32),
+                vmem((tp, 8, mlp), f32), vmem((2, rows, model_dim), bf16), vmem((2 * seq_len, model_dim), bf16), vmem((share, model_dim), bf16), vmem((share, model_dim), f32),
                 dma((layers, 6)), dma((6,)), dma((2,)), dma((2, 2)),
                 dma((images, chips, 2, 2)), dma((images, chips, 2, 2)), dma((images, 2, chips)), dma((images, 2, chips)),
                 dma((chips, 2)), dma((chips, 2)), dma((chips,)), dma((chips,)),

time: 231 us -> 228 us (0.987)
    pallas_call x1, Pallas kernels: 224 us -> 222 us  [per_device(): pl.pallas_call(functools.partial(layers_kernel, seq_len, head_dim, tp, dp...]
where the time goes in v6:
time: 228 us
  Pallas kernels  222 us (97%)
  local copies, waits for them, and re-layouts  6.16 us (3%)
    pallas_call x1, Pallas kernels, per_device(): pl.pallas_call(functools.partial(layers_kernel, seq_len, head_dim, tp, dp...  222 us
    unnamed x1, local copies, waits for them, and re-layouts  6.16 us

profile of v6, /device:TPU:21, one launch (start us, length us, event | category | flops | bytes accessed | tf_op | source)
XLA Modules:
  0.0 228.0 jit_solution(9926154559194100662)
XLA Ops:
  0.0 221.9 %layers.1 = (bf16[8192,1024]{1,0:T(8,128)(2,1)S(1)}, bf16[12288,1024]{1,0:T(8,128)(2,1)}) custom-call(bf16[8192,1024]{1,0:T(8,128)(2,1)} %bitcast.6, bf16[2,64,1024]{2,1,0:T(8,128)(2,1)} %bitcast.7, bf16[2,64,1024]{2,1,0:T(8,128)(2,1)} %bitcast.8, bf16[2,64,1024]{2,1,0:T(8,128)(2,1)} %bitcast.9, bf16[2,1024,256]{2,1,0:T(8,128)(2,1)} %wup_hbm.1, ...), custom_call_target="tpu_custom_call" | custom-call | flops 30064771072 | bytes 67108864 | tf_op jit(solution)/shard_map/layers/pallas_call | solution.py:587
  221.9 6.2 %copy.15 = bf16[32,256,1024]{2,1,0:T(8,128)(2,1)} copy(bf16[32,256,1024]{2,1,0:T(8,128)(2,1)S(1)} %bitcast.5) | data formatting | bytes 33554432

commit v7 on v6

--- a/solution.py
+++ b/solution.py
@@ -91,17 +91,19 @@
     side = max(plane)
     events = {}
     for number in range(1, chips):
-        begin = 4 + ((7 * (number - 1) + 1) // 2 if side < 3 else 3 * (number - 1))
+        begin, lag = 4 + 3 * (number - 1), 0
+        if side < 3 and number > 4:
+            begin, lag = begin + 2 * (number - 5), 1
         if number % 2 == 1:
             pair = (number + 1) // 2
             events.setdefault(begin, []).extend([("came", pair, 0), ("onward", pair, 0)])
             events.setdefault(begin + 2, []).append(("onward", pair, 1))
         events.setdefault(begin, []).append(("pass", number, 0))
         for hop in range(1, side):
-            events.setdefault(begin + 1 + hop, []).append(("line", number, hop))
+            events.setdefault(begin + lag + 1 + hop, []).append(("line", number, hop))
         for hop in range(1, side):
-            events.setdefault(begin + 2 + side + hop, []).append(("plane", number, hop))
-        events.setdefault(begin + 1 + 2 * side, []).append(("pair", number, 0))
+            events.setdefault(begin + lag + 2 + side + hop, []).append(("plane", number, hop))
+        events.setdefault(begin + lag + 1 + 2 * side, []).append(("pair", number, 0))
     return events
 
 
@@ -391,21 +393,26 @@
     ready = [due - 2 * number + 1 for due, due_events in events.items() for kind, number, _ in due_events if kind == "pair"]
     second = max([LEAD + items] + ready)
 
+    period = 2 * (chips - 1)
+
+    def parts_of(image, step, way, sub):
+        @pl.when(sub == 0)
+        def _():
+            pair_arrival(image, way, step).wait_recv()
+
+        span = pl.ds(pl.multiple_of(sub * quarter, quarter), quarter)
+        return from_partner[image, way, step, span].astype(f32) + mine[image, way, step, span].astype(f32)
+
     def turn(index, carry):
         t = index - LEAD
 
-        @pl.when(jnp.logical_and(t >= 0, t < 2 * items))
+        @pl.when(jnp.logical_and(t >= 0, t < images * period))
         def _():
-            image = t // (2 * chips)
-            step = lax.rem(t, 2 * chips) // 2
+            image = t // period
+            step = lax.rem(t, period) // 2
             sub = lax.rem(t, 2)
-            span = pl.ds(pl.multiple_of(sub * quarter, quarter), quarter)
             for way in range(2):
-                @pl.when(sub == 0)
-                def _():
-                    pair_arrival(image, way, step).wait_recv()
-
-                local = from_partner[image, way, step, span].astype(f32) + mine[image, way, step, span].astype(f32)
+                local = parts_of(image, step, way, sub)
 
                 @pl.when(step == 0)
                 def _():
@@ -414,22 +421,22 @@
                 @pl.when(step > 0)
                 def _():
                     ring_copy(image, step - 1, way, sub).wait_recv()
-
-                @pl.when(jnp.logical_and(step > 0, step < chips - 1))
-                def _():
                     ring[image, step, way, sub] = (ring[image, step, way, sub].astype(f32) + local).astype(ring.dtype)
 
-                @pl.when(step < chips - 1)
-                def _():
-                    ring_copy(image, step, way, sub).start()
-
-                @pl.when(step == chips - 1)
-                def _():
-                    here = pl.ds(pl.multiple_of(image * seq_len + way * half + sub * quarter, quarter), quarter)
-                    total = ring[image, chips - 1, way, sub].astype(f32) + local
-                    middle = (own_x[here].astype(f32) + bias_rows[0] + total).astype(jnp.bfloat16).astype(f32)
-                    h_ref[here] = norm_rows(middle, ln_rows[1])
-                    acc_ref[here] = middle + bias_rows[1]
+                ring_copy(image, step, way, sub).start()
+
+        @pl.when(jnp.logical_and(t >= period, jnp.logical_and(t < images * period + 2, lax.rem(t + period, period) < 2)))
+        def _():
+            image = t // period - 1
+            sub = lax.rem(t, 2)
+            for way in range(2):
+                local = parts_of(image, chips - 1, way, sub)
+                ring_copy(image, chips - 2, way, sub).wait_recv()
+                here = pl.ds(pl.multiple_of(image * seq_len + way * half + sub * quarter, quarter), quarter)
+                total = ring[image, chips - 1, way, sub].astype(f32) + local
+                middle = (own_x[here].astype(f32) + bias_rows[0] + total).astype(jnp.bfloat16).astype(f32)
+                h_ref[here] = norm_rows(middle, ln_rows[1])
+                acc_ref[here] = middle + bias_rows[1]
 
         for due, due_events in sorted(events.items()):
             @pl.when(index == due)

time: 228 us -> 227 us (level)
  no operation moved by 1% of the time
where the time goes in v7:
time: 227 us
  Pallas kernels  220 us (97%)
  local copies, waits for them, and re-layouts  6.16 us (3%)
    pallas_call x1, Pallas kernels, per_device(): pl.pallas_call(functools.partial(layers_kernel, seq_len, head_dim, tp, dp...  220 us
    unnamed x1, local copies, waits for them, and re-layouts  6.16 us

profile of v7, /device:TPU:21, one launch (start us, length us, event | category | flops | bytes accessed | tf_op | source)
XLA Modules:
  0.0 226.6 jit_solution(3748388109324570249)
XLA Ops:
  0.0 220.4 %layers.1 = (bf16[8192,1024]{1,0:T(8,128)(2,1)S(1)}, bf16[12288,1024]{1,0:T(8,128)(2,1)}) custom-call(bf16[8192,1024]{1,0:T(8,128)(2,1)} %bitcast.6, bf16[2,64,1024]{2,1,0:T(8,128)(2,1)} %bitcast.7, bf16[2,64,1024]{2,1,0:T(8,128)(2,1)} %bitcast.8, bf16[2,64,1024]{2,1,0:T(8,128)(2,1)} %bitcast.9, bf16[2,1024,256]{2,1,0:T(8,128)(2,1)} %wup_hbm.1, ...), custom_call_target="tpu_custom_call" | custom-call | flops 30064771072 | bytes 67108864 | tf_op jit(solution)/shard_map/layers/pallas_call | solution.py:594
  220.4 6.2 %copy.15 = bf16[32,256,1024]{2,1,0:T(8,128)(2,1)} copy(bf16[32,256,1024]{2,1,0:T(8,128)(2,1)S(1)} %bitcast.5) | data formatting | bytes 33554432

commit v8 on v7

--- a/solution.py
+++ b/solution.py
@@ -123,7 +123,7 @@
     qkv = 3 * head_dim
     share = own_x.shape[0]
     images = share // seq_len
-    quarter = seq_len // 4
+    eighth = seq_len // 8
     half = seq_len // 2
     f32 = jnp.float32
     plane = plane_of(dp)
@@ -306,8 +306,8 @@
         return core + odd - 2 * core * odd
 
     def chunk(image, way, sub, owner):
-        offset = owner * share + image * seq_len + way * (2 * quarter) + sub * quarter
-        return out_ref.at[pl.ds(pl.multiple_of(offset, quarter), quarter)]
+        offset = owner * share + image * seq_len + way * half + sub * eighth
+        return out_ref.at[pl.ds(pl.multiple_of(offset, eighth), eighth)]
 
     def origin(way, step):
         back = chip - step if way == 0 else chip + step
@@ -336,15 +336,16 @@
 
     def event(image, number):
         step = number // 2
-        sub = lax.rem(number, 2)
-        for way in range(2):
-            arrival(image, way, sub, step).wait_recv()
-
-            @pl.when(step + 1 < chips - 1)
-            def _():
-                out_copy(image, way, sub, step + 1).start()
-
-            out_pair(image, way, sub, step + 1, core).start()
+        for fine in range(2):
+            sub = 2 * lax.rem(number, 2) + fine
+            for way in range(2):
+                arrival(image, way, sub, step).wait_recv()
+
+                @pl.when(step + 1 < chips - 1)
+                def _():
+                    out_copy(image, way, sub, step + 1).start()
+
+                out_pair(image, way, sub, step + 1, core).start()
 
     peers = [("tp", right), ("tp", left), ("tp", partner)]
     for axis in range(2):
@@ -400,7 +401,7 @@
         def _():
             pair_arrival(image, way, step).wait_recv()
 
-        span = pl.ds(pl.multiple_of(sub * quarter, quarter), quarter)
+        span = pl.ds(pl.multiple_of(sub * eighth, eighth), eighth)
         return from_partner[image, way, step, span].astype(f32) + mine[image, way, step, span].astype(f32)
 
     def turn(index, carry):
@@ -410,33 +411,35 @@
         def _():
             image = t // period
             step = lax.rem(t, period) // 2
-            sub = lax.rem(t, 2)
-            for way in range(2):
-                local = parts_of(image, step, way, sub)
-
-                @pl.when(step == 0)
-                def _():
-                    ring[image, 0, way, sub] = local.astype(ring.dtype)
-
-                @pl.when(step > 0)
-                def _():
-                    ring_copy(image, step - 1, way, sub).wait_recv()
-                    ring[image, step, way, sub] = (ring[image, step, way, sub].astype(f32) + local).astype(ring.dtype)
-
-                ring_copy(image, step, way, sub).start()
+            for fine in range(2):
+                sub = 2 * lax.rem(t, 2) + fine
+                for way in range(2):
+                    local = parts_of(image, step, way, sub)
+
+                    @pl.when(step == 0)
+                    def _():
+                        ring[image, 0, way, sub] = local.astype(ring.dtype)
+
+                    @pl.when(step > 0)
+                    def _():
+                        ring_copy(image, step - 1, way, sub).wait_recv()
+                        ring[image, step, way, sub] = (ring[image, step, way, sub].astype(f32) + local).astype(ring.dtype)
+
+                    ring_copy(image, step, way, sub).start()
 
         @pl.when(jnp.logical_and(t >= period, jnp.logical_and(t < images * period + 2, lax.rem(t + period, period) < 2)))
         def _():
             image = t // period - 1
-            sub = lax.rem(t, 2)
-            for way in range(2):
-                local = parts_of(image, chips - 1, way, sub)
-                ring_copy(image, chips - 2, way, sub).wait_recv()
-                here = pl.ds(pl.multiple_of(image * seq_len + way * half + sub * quarter, quarter), quarter)
-                total = ring[image, chips - 1, way, sub].astype(f32) + local
-                middle = (own_x[here].astype(f32) + bias_rows[0] + total).astype(jnp.bfloat16).astype(f32)
-                h_ref[here] = norm_rows(middle, ln_rows[1])
-                acc_ref[here] = middle + bias_rows[1]
+            for fine in range(2):
+                sub = 2 * lax.rem(t, 2) + fine
+                for way in range(2):
+                    local = parts_of(image, chips - 1, way, sub)
+                    ring_copy(image, chips - 2, way, sub).wait_recv()
+                    here = pl.ds(pl.multiple_of(image * seq_len + way * half + sub * eighth, eighth), eighth)
+                    total = ring[image, chips - 1, way, sub].astype(f32) + local
+                    middle = (own_x[here].astype(f32) + bias_rows[0] + total).astype(jnp.bfloat16).astype(f32)
+                    h_ref[here] = norm_rows(middle, ln_rows[1])
+                    acc_ref[here] = middle + bias_rows[1]
 
         for due, due_events in sorted(events.items()):
             @pl.when(index == due)
@@ -512,10 +515,10 @@
             @pl.when(shard == tp - 1)
             def _():
                 out_ref[pl.ds(pl.multiple_of(me * share + image * seq_len, seq_len), seq_len)] = acc_ref[span].astype(out_ref.dtype)
-                for sub in range(2):
+                for sub in range(4):
                     for way in range(2):
                         out_copy(image, way, sub, 0).start()
-                for sub in range(2):
+                for sub in range(4):
                     for way in range(2):
                         out_pair(image, way, sub, 0, core).start()
 
@@ -538,7 +541,7 @@
     def drain(step, carry):
         for image in range(images):
             for way in range(2):
-                for sub in range(2):
+                for sub in range(4):
                     @pl.when(step < chips - 1)
                     def _():
                         ring_copy(image, step, way, sub).wait_send()
@@ -582,7 +585,7 @@
         mlp = w_up.shape[2]
         share = n_tokens // tp
         images = share // seq_len
-        half, quarter = seq_len // 2, seq_len // 4
+        half, eighth = seq_len // 2, seq_len // 8
         rows = 4 * head_dim + 2 * mlp
         side = max(plane_of(dp))
         bf16, f32 = jnp.bfloat16, jnp.float32
@@ -600,15 +603,15 @@
                 vmem((layers, model_dim), bf16), vmem((layers, model_dim), bf16), vmem((layers, model_dim), bf16), vmem((layers, mlp), bf16), vmem((layers, head_dim), bf16), vmem((layers, head_dim), bf16),
                 vmem((layers, rows, model_dim), bf16), vmem((layers, model_dim, mlp), bf16),
                 vmem((2, 2 * seq_len, model_dim), bf16), vmem((share, model_dim), bf16),
-                vmem((images, chips, 2, 2, quarter, model_dim), bf16),
+                vmem((images, chips, 2, 4, eighth, model_dim), bf16),
                 vmem((images, 2, chips, half, model_dim), bf16), vmem((4, 2, half, model_dim), bf16), vmem((images, 2, chips, half, model_dim), bf16),
                 vmem((tp, 8, mlp), f32), vmem((2, rows, model_dim), bf16), vmem((2 * seq_len, model_dim), bf16), vmem((share, model_dim), bf16), vmem((share, model_dim), f32),
                 dma((layers, 6)), dma((6,)), dma((2,)), dma((2, 2)),
-                dma((images, chips, 2, 2)), dma((images, chips, 2, 2)), dma((images, 2, chips)), dma((images, 2, chips)),
+                dma((images, chips, 2, 4)), dma((images, chips, 2, 4)), dma((images, 2, chips)), dma((images, 2, chips)),
                 dma((chips, 2)), dma((chips, 2)), dma((chips,)), dma((chips,)),
                 dma((chips, 2, side)), dma((chips, 2, side)), dma((chips, 2, side, side)), dma((chips, 2, side, side)),
                 dma((chips,)), dma((chips,)), dma((chips,)), dma((chips,)), dma((2,)),
-                dma((images, 2, 2, chips)), dma((images, 2, 2, chips)), dma((images, 2, 2, chips)), dma((images, 2, 2, chips)),
+                dma((images, 2, 4, chips)), dma((images, 2, 4, chips)), dma((images, 2, 4, chips)), dma((images, 2, 4, chips)),
             ],
             compiler_params=pltpu.CompilerParams(vmem_limit_bytes=VMEM_BYTES, collective_id=0, has_side_effects=True),
             cost_estimate=pl.CostEstimate(flops=4 * n_tokens * model_dim * (rows + seq_len // 2), bytes_accessed=8 * n_tokens * model_dim, transcendentals=0),

time: 227 us -> 230 us (1.013)
  Pallas kernels: 220 us -> 224 us
    pallas_call x1, Pallas kernels: 220 us -> 224 us  [per_device(): pl.pallas_call(functools.partial(layers_kernel, seq_len, head_dim, tp, dp...]
where the time goes in v8:
time: 230 us
  Pallas kernels  224 us (97%)
  local copies, waits for them, and re-layouts  6.16 us (3%)
    pallas_call x1, Pallas kernels, per_device(): pl.pallas_call(functools.partial(layers_kernel, seq_len, head_dim, tp, dp...  224 us
    unnamed x1, local copies, waits for them, and re-layouts  6.16 us

profile of v8, /device:TPU:21, one launch (start us, length us, event | category | flops | bytes accessed | tf_op | source)
XLA Modules:
  0.0 229.7 jit_solution(9041178431191150259)
XLA Ops:
  0.0 223.5 %layers.1 = (bf16[8192,1024]{1,0:T(8,128)(2,1)S(1)}, bf16[12288,1024]{1,0:T(8,128)(2,1)}) custom-call(bf16[8192,1024]{1,0:T(8,128)(2,1)} %bitcast.6, bf16[2,64,1024]{2,1,0:T(8,128)(2,1)} %bitcast.7, bf16[2,64,1024]{2,1,0:T(8,128)(2,1)} %bitcast.8, bf16[2,64,1024]{2,1,0:T(8,128)(2,1)} %bitcast.9, bf16[2,1024,256]{2,1,0:T(8,128)(2,1)} %wup_hbm.1, ...), custom_call_target="tpu_custom_call" | custom-call | flops 30064771072 | bytes 67108864 | tf_op jit(solution)/shard_map/layers/pallas_call | solution.py:597
  223.6 6.2 %copy.15 = bf16[32,256,1024]{2,1,0:T(8,128)(2,1)} copy(bf16[32,256,1024]{2,1,0:T(8,128)(2,1)S(1)} %bitcast.5) | data formatting | bytes 33554432
